TPU v7x, 256 devices: a whole 4x4x8 slice. The times are simulated.
256 devices in a mesh: grp: 4 (over y), col: 64 (over x, z, core).
Axes of the slice: x: 4, y: 4, z: 8, core: 2. Of those that a mesh axis runs over, the one named last changes fastest.
Arguments:
- panels: bfloat16 [256, 4, 512, 512], P('col', None, 'grp'), may hold values from -1.296875 to 1.296875
- parent: float32 [256, 512, 512], P('col', 'grp'), may hold values from -6 to 6
- src_block: int32 [64, 40], P('col'), may hold values from 0 to 39, each once within a row
- dest_owner: int32 [2560, 1], P('col'), may hold values from 0 to 63; in each aligned block of 40 rows (0 to 39, 40 to 79, ...) no two rows name the same one
- target: int32 [2560], P('col'), may hold values from 0 to 3
- counts: int32 [64], P('col'), may hold values from 20 to 40, as said below
Outputs:
- assembled: float32 [256, 512, 512], P('col', 'grp')
Inputs may be any that keep to these rules, and one draw needn't show every extreme that they name: `src_block`: each row of a column rank is a permutation of the 40 block pairs. `dest_owner`: among the 40 slots of one column rank at most 1 name the same owner. The live slots of a rank are its first counts[c]; some rank has all 40 live.
All inputs are finite; a program needn't handle non-finite values.
Results may differ from a plain program's by a relative error of at most 0.0026.
Values may be sent and summed in bfloat16 or wider, within the bound.
A program may use at most 128 MiB of HBM per device.

v0:
```python
import functools

import jax
import jax.numpy as jnp
import numpy as np
from jax import lax
from jax.experimental import pallas as pl
from jax.experimental.pallas import tpu as pltpu
from jax.sharding import PartitionSpec as P

MESH = pl.DeviceIdType.MESH


def place_slots(src_block, dest_owner, target, counts, peer_count, capacity):
    slot_count = src_block.shape[1]
    slot_index = jnp.arange(slot_count, dtype=jnp.int32)
    owner_rank = dest_owner[:, 0]
    matches = (owner_rank[:, None] == jnp.arange(peer_count, dtype=jnp.int32)[None, :]).astype(
        jnp.int32
    )
    earlier = jnp.cumsum(matches, axis=0) - matches
    rank_in = jnp.sum(earlier * matches, axis=1)
    position = owner_rank * capacity + rank_in
    is_live = slot_index < counts[0]
    routed = jnp.zeros((peer_count * capacity,), jnp.int32).at[position].set(target)
    return (src_block[0], position, is_live, routed.reshape(peer_count, capacity))


def pack_updates(flat_updates, chosen, position, is_live, peer_count, capacity):
    picked = flat_updates[chosen]
    picked = jnp.where(is_live[:, None, None], picked, jnp.zeros_like(picked))
    buffer = (
        jnp.zeros((peer_count * capacity,) + picked.shape[1:], picked.dtype)
        .at[position]
        .set(picked)
    )
    return buffer.reshape((peer_count, capacity) + picked.shape[1:])


def assemble(received, labels, targets):
    arrived = received.reshape((-1,) + received.shape[2:])
    flat_labels = labels.reshape(-1)
    select = (flat_labels[None, :] == jnp.arange(targets, dtype=jnp.int32)[:, None]).astype(
        jnp.bfloat16
    )
    return jnp.einsum("tn,nrc->trc", select, arrived, preferred_element_type=jnp.float32)


def pair_products(own_rows, piece_rows):
    blocks = own_rows.shape[1]
    upper_table = np.array([a for a in range(blocks) for b in range(a + 1)], np.int32)
    lower_table = np.array([b for a in range(blocks) for b in range(a + 1)], np.int32)
    left_rows = own_rows[:, upper_table]
    right_rows = piece_rows[:, lower_table]
    return jnp.einsum(
        "fprw,fpcw->fprc", left_rows, right_rows, preferred_element_type=jnp.float32
    ).astype(jnp.bfloat16)


def kernel(
    chips, capacity, split, src_block, owner, target, counts, own, parent, out,
    table, from_x, from_y, product, kept, summed, to_pair, from_pair, to_chip, from_chip,
    to_back, from_back,
    x_send, x_recv, y_send, y_recv, p_send, p_recv, z_send, z_recv, b_send, b_recv,
):
    fronts, blocks, quarter, width = own.shape
    targets = parent.shape[0]
    pairs = blocks * (blocks + 1) // 2
    slots = src_block.shape[1]
    g, c = lax.axis_index("grp"), lax.axis_index("col")
    gy, gx = g // 2, g % 2
    z, core = c // 2, c % 2
    x_peer = gy * 2 + (1 - gx)
    y_peer = (1 - gy) * 2 + gx
    d_peer = 3 - g
    to_x, to_y = {"grp": x_peer, "col": c}, {"grp": y_peer, "col": c}
    to_core = {"grp": g, "col": z * 2 + 1 - core}
    far = [lax.rem(z + hop, chips) for hop in range(1, chips)]
    to_far = [{"grp": g, "col": chip * 2 + core} for chip in far]

    barrier = pltpu.get_barrier_semaphore()
    peers = [to_x, to_y, to_core] + to_far
    for peer in peers:
        pl.semaphore_signal(barrier, inc=1, device_id=peer, device_id_type=MESH)
    pl.semaphore_wait(barrier, len(peers))

    def remote(src, dst, send, recv, device):
        return pltpu.make_async_remote_copy(
            src_ref=src, dst_ref=dst, send_sem=send, recv_sem=recv,
            device_id=device, device_id_type=MESH,
        )

    piece = quarter // split
    x_copy, y_copy = [], []
    for k in range(split):
        at = pl.ds(k * piece, piece)
        x_copy.append(
            remote(own.at[:, :, at], from_x[k], x_send.at[k], x_recv.at[k], to_x)
        )
        y_copy.append(
            remote(own.at[:, :, at], from_y[k], y_send.at[k], y_recv.at[k], to_y)
        )
        x_copy[k].start()
        y_copy[k].start()

    def list_owner(o, carry):
        def look(s, state):
            count, chosen, label = state
            mine = owner[0, s] == o
            named = jnp.where(s < counts[0], target[0, s] + 1, 0)
            hits = [jnp.logical_and(mine, count == k) for k in range(capacity)]
            return (
                count + jnp.where(mine, 1, 0),
                tuple(jnp.where(hits[k], src_block[0, s], chosen[k]) for k in range(capacity)),
                tuple(jnp.where(hits[k], named, label[k]) for k in range(capacity)),
            )

        none = tuple(jnp.int32(0) for _ in range(capacity))
        _, chosen, label = lax.fori_loop(0, slots, look, (jnp.int32(0), none, none))
        for k in range(capacity):
            table[0, o * capacity + k] = chosen[k]
            table[1, o * capacity + k] = label[k]
        return carry

    lax.fori_loop(0, 2 * chips, list_owner, 0)

    def place(n, source, against, pieces):
        high = quarter // pieces
        share = len(source) // pieces
        return [
            (source[i * share:(i + 1) * share], high, against, n * quarter + i * high)
            for i in range(pieces)
        ]

    units = (
        place(0, [own], [own], 1)
        + [
            ([from_x[k], from_y[k]], 2 * piece, [own], quarter + k * 2 * piece)
            for k in range(split)
        ]
        + place(3, from_y, from_x, 2)
    )
    u_own, u_near, u_d = 0, list(range(1, 1 + split)), [1 + split, 2 + split]
    tile = 32

    p_copy, z_copy = [], []
    for u in range(len(units)):
        p_copy.append(remote(to_pair[u], from_pair[u], p_send.at[u], p_recv.at[u], to_core))
        z_copy.append([
            remote(
                to_chip[u].at[h], from_chip[u].at[h],
                z_send.at[u, h], z_recv.at[u, h], to_far[h],
            )
            for h in range(chips - 1)
        ])

    def select(high, parity, store):
        def chip(zz, carry):
            base = (zz * 2 + parity) * capacity
            chosen = [table[0, base + k] for k in range(capacity)]
            label = [table[1, base + k] for k in range(capacity)]
            weight = [
                [jnp.where(label[k] == t + 1, 1.0, 0.0).astype(jnp.float32) for t in range(targets)]
                for k in range(capacity)
            ]

            def rows(i, carry):
                start = pl.multiple_of(i * tile, tile)
                taken = [
                    product[chosen[k], pl.ds(start, tile), :].astype(jnp.float32)
                    for k in range(capacity)
                ]
                for t in range(targets):
                    total = taken[0] * weight[0][t]
                    for k in range(1, capacity):
                        total = total + taken[k] * weight[k][t]
                    store(zz, t, start, total)
                return carry

            return lax.fori_loop(0, high // tile, rows, carry)

        lax.fori_loop(0, chips, chip, 0)

    def make(u):
        source, high, against, _ = units[u]

        def front(f, carry):
            for b in range(blocks):
                left = jnp.concatenate([ref[f, b] for ref in source], axis=0)
                right = jnp.concatenate(
                    [ref[f, a] for a in range(b, blocks) for ref in against], axis=0
                )
                made = lax.dot_general(
                    left, right, (((1,), (1,)), ((), ())),
                    preferred_element_type=jnp.float32,
                ).astype(jnp.bfloat16)
                for a in range(b, blocks):
                    at = f * pairs + a * (a + 1) // 2 + b
                    product[at, :high] = made[:, (a - b) * quarter:(a - b + 1) * quarter]
            return carry

        lax.fori_loop(0, fronts, front, 0)

        def store_pair(zz, t, start, total):
            to_pair[u][zz, t, pl.ds(start, tile), :] = total.astype(jnp.bfloat16)

        def store_kept(zz, t, start, total):
            kept[zz, t, pl.ds(start, tile), :] = total

        select(high, 1 - core, store_pair)
        p_copy[u].start()
        select(high, core, store_kept)

    def pass_on(u):
        _, high, _, row = units[u]
        at = slice(row, row + high)
        p_copy[u].wait_recv()
        for h in range(chips - 1):
            to_chip[u][h] = (
                kept[far[h], :, :high] + from_pair[u][far[h]].astype(jnp.float32)
            ).astype(jnp.bfloat16)
            z_copy[u][h].start()
        summed[:, at] = kept[z, :, :high] + from_pair[u][z].astype(jnp.float32)

    def finish(u):
        _, high, _, row = units[u]
        at = slice(row, row + high)
        for h in range(chips - 1):
            z_copy[u][h].wait_recv()
        total = summed[:, at]
        for h in range(chips - 1):
            total = total + from_chip[u][h].astype(jnp.float32)
        return total

    def settle(u):
        _, high, _, row = units[u]
        summed[:, row:row + high] = finish(u)

    def write(member, total_of):
        at = pl.ds(pl.multiple_of(member * quarter, quarter), quarter)
        for t in range(targets):
            out[t, :, at] = parent[t, :, at] - total_of(t).T

    def near(first):
        parts = [slice(units[u][3] + first, units[u][3] + first + piece) for u in u_near]
        return lambda t: jnp.concatenate([summed[t, part] for part in parts], axis=0)

    make(u_own)
    pass_on(u_own)
    for k in range(split - 1):
        x_copy[k].wait_recv()
        y_copy[k].wait_recv()
        make(u_near[k])
        pass_on(u_near[k])
    settle(u_own)
    write(g, lambda t: summed[t, :quarter])
    x_copy[-1].wait_recv()
    y_copy[-1].wait_recv()
    for u in u_d + u_near[-1:]:
        make(u)
        pass_on(u)
    for k in range(split - 1):
        settle(u_near[k])
    back = []
    for i, u in enumerate(u_d):
        to_back[i][...] = finish(u)
        back.append(remote(to_back[i], from_back[i], b_send.at[i], b_recv.at[i], to_x))
        back[i].start()
    settle(u_near[-1])
    write(x_peer, near(0))
    write(y_peer, near(piece))
    for copy in back:
        copy.wait_recv()
    write(d_peer, lambda t: jnp.concatenate([ref[t] for ref in from_back], axis=0))
    for copy in x_copy + y_copy + p_copy + back:
        copy.wait_send()
    for row in z_copy:
        for copy in row:
            copy.wait_send()


def fused(panels, parent, src_block, dest_owner, target, counts, chips, capacity):
    fronts, blocks, quarter, width = panels.shape
    targets = parent.shape[0]
    pairs = blocks * (blocks + 1) // 2
    split = 4
    units = 3 + split
    piece = pltpu.VMEM((fronts, blocks, quarter // split, width), panels.dtype)
    heights = [quarter] + [2 * quarter // split] * split + [quarter // 2] * 2

    def buffers(count):
        return [pltpu.VMEM((count, targets, high, quarter), jnp.bfloat16) for high in heights]

    last = (targets, quarter, quarter)
    half = pltpu.VMEM((targets, quarter // 2, quarter), jnp.float32)
    dma = pltpu.SemaphoreType.DMA
    scalars = pl.BlockSpec(memory_space=pltpu.SMEM)
    arrays = pl.BlockSpec(memory_space=pltpu.VMEM)
    return pl.pallas_call(
        functools.partial(kernel, chips, capacity, split),
        out_shape=jax.ShapeDtypeStruct(parent.shape, parent.dtype),
        in_specs=[scalars] * 4 + [arrays] * 2,
        out_specs=arrays,
        scratch_shapes=[
            pltpu.SMEM((2, 2 * chips * capacity), jnp.int32),
            [piece] * split, [piece] * split,
            pltpu.VMEM((fronts * pairs, quarter, quarter), jnp.bfloat16),
            pltpu.VMEM((chips,) + last, jnp.float32),
            pltpu.VMEM((targets, 4 * quarter, quarter), jnp.float32),
            buffers(chips), buffers(chips), buffers(chips - 1), buffers(chips - 1),
            [half, half], [half, half],
            dma((split,)), dma((split,)), dma((split,)), dma((split,)),
            dma((units,)), dma((units,)), dma((units, chips - 1)), dma((units, chips - 1)),
            dma((2,)), dma((2,)),
        ],
        compiler_params=pltpu.CompilerParams(
            collective_id=0, has_side_effects=True, vmem_limit_bytes=60 * 1024 * 1024
        ),
    )(src_block, dest_owner.reshape(1, -1), target.reshape(1, -1), counts, panels, parent)


def per_device(panels, parent, src_block, dest_owner, target, counts):
    fronts, blocks, quarter, _ = panels.shape
    pair_count = blocks * (blocks + 1) // 2
    peer_count = lax.axis_size("col")
    slot_count = src_block.shape[1]
    capacity = (slot_count + peer_count - 1) // peer_count + slot_count // (2 * peer_count)
    targets = parent.shape[0]
    if lax.axis_size("grp") == 4 and peer_count % 2 == 0 and targets < capacity:
        return fused(
            panels, parent, src_block, dest_owner, target, counts, peer_count // 2, capacity
        )
    chosen, position, is_live, routed = place_slots(
        src_block, dest_owner, target, counts, peer_count, capacity
    )
    products = pair_products(panels, lax.all_gather(panels, "grp", axis=2, tiled=True))
    flat_updates = products.reshape(fronts * pair_count, quarter, products.shape[3])
    buffer = pack_updates(flat_updates, chosen, position, is_live, peer_count, capacity)
    received, labels = (
        lax.all_to_all(buffer, "col", split_axis=0, concat_axis=0, tiled=True),
        lax.all_to_all(routed, "col", split_axis=0, concat_axis=0, tiled=True),
    )
    return parent - assemble(received, labels, targets)


def solution(mesh):
    placed = (
        P("col", None, "grp", None),
        P("col", "grp", None),
        P("col", None),
        P("col", None),
        P("col"),
        P("col"),
    )
    return jax.shard_map(
        per_device, mesh=mesh, in_specs=placed, out_specs=P("col", "grp", None), check_vma=False
    )
```

profile of v0, /device:TPU:8, one launch (start us, length us, event | category | flops | bytes accessed | tf_op | source)
XLA Modules:
  0.0 388.6 jit_solution(11302547754613624316)
XLA Ops:
  6.5 0.0 copy-start.1
  6.5 0.0 copy-start.2
  6.5 0.0 all-gather.2.cloned.1.call-start
  6.5 0.7 all-gather.2.cloned.1.call-update
  7.3 0.7 fusion.13
  8.0 0.1 reduce_window_sum.11
  8.1 0.8 select_reduce_fusion
  8.9 0.7 fusion.17
  9.6 0.8 scatter_custom_fusion
  10.4 0.7 copy.36
  11.1 11.9 %all-to-all-start = ((s32[64,1,1]{2,1,0:T(1,128)}), s32[64,1,1]{2,1,0:T(1,128)S(1)}, u32[]{:S(2)}, u32[]{:S(2)}) async-start(s32[64,1,1]{2,1,0:T(1,128)} %copy.36), calls=%async_computation | async-start | bytes 65536 | tf_op jit(solution)/shard_map/all_to_all | solution.py:341
  23.0 0.7 pad_clamp_fusion.2
  23.7 5.7 %gather_fusion = bf16[10,4,128,512]{3,2,1,0:T(8,128)(2,1)} fusion(bf16[4,4,128,512]{3,2,1,0:T(8,128)(2,1)} %param.10, s32[1024]{0:T(1024)S(1)} %pad_clamp_fusion.2), kind=kCustom, calls=%fused_computation | custom fusion | bytes 10485800 | tf_op jit(solution)/shard_map/gather | solution.py:53
  30.1 0.0 copy-done.1
  30.1 0.0 copy-done.2
  30.1 67.5 %all-gather.2.cloned.1.call-done = bf16[4,4,512,512]{3,2,1,0:T(8,128)(2,1)} async-done(((bf16[4,4,128,512]{3,2,1,0:T(8,128)(2,1)}), bf16[4,4,512,512]{3,2,1,0:T(8,128)(2,1)}) %all-gather.2.cloned.1.call-update) | async-done | bytes 8388624 | tf_op jit(solution)/shard_map/all_gather | solution.py:336
  97.7 6.0 %fusion.22 = (bf16[4,4,256,512]{3,2,1,0:T(8,128)(2,1)}, bf16[4,4,256,512]{3,2,1,0:T(8,128)(2,1)}) fusion(bf16[4,4,512,512]{3,2,1,0:T(8,128)(2,1)} %all-gather.2.cloned.1.call-done), kind=kLoop, calls=%fused_computation.37 | loop fusion | bytes 16777216 | tf_op jit(solution)/shard_map/gather | solution.py:54
  103.7 7.6 %gather_fusion.2 = bf16[10,4,256,512]{3,2,1,0:T(8,128)(2,1)} fusion(bf16[4,4,256,512]{3,2,1,0:T(8,128)(2,1)} %get-tuple-element.5, s32[1024]{0:T(1024)S(1)} %pad_clamp_fusion.1), kind=kCustom, calls=%fused_computation.2 | custom fusion | bytes 20971560 | tf_op jit(solution)/shard_map/gather | solution.py:54
  111.3 0.0 slice-start
  111.3 7.7 %gather_fusion.3 = bf16[10,4,256,512]{3,2,1,0:T(8,128)(2,1)} fusion(bf16[4,4,256,512]{3,2,1,0:T(8,128)(2,1)} %get-tuple-element.6, s32[1024]{0:T(1024)S(1)} %pad_clamp_fusion.1), kind=kCustom, calls=%fused_computation.3 | custom fusion | bytes 20971560 | tf_op jit(solution)/shard_map/gather | solution.py:54
  119.0 0.0 slice-start.1
  119.0 12.3 %copy_bitcast_fusion = (bf16[4,10,256,512]{3,2,1,0:T(8,128)(2,1)S(1)}, bf16[4,10,256,512]{3,2,1,0:T(8,128)(2,1)}) fusion(bf16[10,4,256,512]{3,2,1,0:T(8,128)(2,1)} %gather_fusion.3, bf16[10,4,256,512]{3,2,1,0:T(8,128)(2,1)} %gather_fusion.2), kind=kLoop, calls=%fused_computation.10 | loop fusion | bytes 41943040 | tf_op jit(solution)/shard_map/gather | solution.py:54
  131.3 0.0 slice-done
  131.3 0.0 slice-done.1
  131.3 10.5 %fusion.8 = bf16[4,10,128,512]{3,2,1,0:T(8,128)(2,1)} fusion(bf16[4,10,256,512]{3,2,1,0:T(8,128)(2,1)S(1)} %get-tuple-element.7, bf16[4,10,256,512]{3,2,1,0:T(8,128)(2,1)} %get-tuple-element.8, bf16[10,4,128,512]{3,2,1,0:T(8,128)(2,1)S(1)} %bitcast.34), kind=kOutput, calls=%fused_computation.17 | convolution fusion | flops 2728919040 | bytes 31457280 | tf_op jit(solution)/shard_map/fprw,fpcw->fprc/dot_general | solution.py:55
  141.8 7.2 %gather_fusion.1 = bf16[40,128,512]{2,1,0:T(8,128)(2,1)} fusion(bf16[40,128,512]{2,1,0:T(8,128)(2,1)} %bitcast.35, s32[1024]{0:T(1024)S(1)} %pad_clamp_fusion), kind=kCustom, calls=%fused_computation.1 | custom fusion | bytes 10485920 | tf_op jit(solution)/shard_map/gather | solution.py:30
  149.0 5.3 %broadcast_select_fusion = bf16[40,128,512]{2,1,0:T(8,128)(2,1)} fusion(bf16[40,128,512]{2,1,0:T(8,128)(2,1)} %gather_fusion.1, pred[40]{0:T(512)(128)(4,1)S(1)} %iota_compare_fusion.2), kind=kLoop, calls=%fused_computation.16 | loop fusion | flops 2621440 | bytes 10485800 | tf_op jit(solution)/shard_map/jit(_where)/select_n | solution.py:31
  154.3 4.2 %broadcast_in_dim.30 = bf16[64,128,512]{2,1,0:T(8,128)(2,1)} broadcast(bf16[]{:T(256)} %constant.10.clone.1), dimensions={} | broadcast | bytes 8388610 | tf_op jit(solution)/shard_map/broadcast_in_dim | solution.py:33
  158.5 14.1 %scatter_fusion = bf16[64,128,512]{2,1,0:T(8,128)(2,1)} fusion(bf16[64,128,512]{2,1,0:T(8,128)(2,1)} %broadcast_in_dim.30, s32[40]{0:T(128)S(1)} %fusion.17, bf16[40,128,512]{2,1,0:T(8,128)(2,1)} %broadcast_select_fusion), kind=kCustom, calls=%fused_computation.5 | custom fusion | bytes 15728800 | tf_op jit(solution)/shard_map/scatter | solution.py:35
  172.6 0.0 all-to-all-done
  172.6 10.9 %all-to-all-start.1 = ((bf16[64,1,128,512]{3,2,1,0:T(8,128)(2,1)}), bf16[64,1,128,512]{3,2,1,0:T(8,128)(2,1)}, u32[]{:S(2)}, u32[]{:S(2)}) async-start(bf16[64,1,128,512]{3,2,1,0:T(8,128)(2,1)} %bitcast.32), calls=%async_computation.1 | async-start | bytes 16777216 | tf_op jit(solution)/shard_map/all_to_all | solution.py:340
  183.5 0.0 copy-start
  183.5 1.2 reduce
  184.7 183.4 %all-to-all-done.1 = bf16[64,1,128,512]{3,2,1,0:T(8,128)(2,1)} async-done(((bf16[64,1,128,512]{3,2,1,0:T(8,128)(2,1)}), bf16[64,1,128,512]{3,2,1,0:T(8,128)(2,1)}, u32[]{:S(2)}, u32[]{:S(2)}) %all-to-all-start.1) | async-done | bytes 8388640 | tf_op jit(solution)/shard_map/all_to_all | solution.py:340
  368.1 12.3 %fusion.4 = f32[4,128,512]{2,0,1:T(4,128)S(1)} fusion(bf16[64,1,128,512]{3,2,1,0:T(8,128)(2,1)} %all-to-all-done.1, s32[64]{0:T(128)S(1)} %reduce), kind=kOutput, calls=%fused_computation.12 | convolution fusion | flops 33554688 | bytes 9437440 | tf_op jit(solution)/shard_map/tn,nrc->trc/dot_general | solution.py:46
  380.4 0.0 copy-done
  380.4 1.4 copy_subtract_fusion
  (5 shorter events, 0.0 us)
Async XLA Ops:
  6.5 23.6 %copy-start.1 = (s32[10]{0:T(128)S(1)}, s32[10]{0:T(128)}, u32[]{:S(2)}) copy-start(s32[10]{0:T(128)} %constant.35) | copy-start | bytes 124
  6.5 23.6 %copy-start.2 = (s32[1,40]{1,0:T(1,128)S(1)}, s32[1,40]{1,0:T(1,128)}, u32[]{:S(2)}) copy-start(s32[1,40]{1,0:T(1,128)} %param.12) | copy-start | bytes 484
  6.5 91.1 %all-gather.2.cloned.1.call-start = ((), (), s32[]{:S(2)}) async-start(), calls=%async_computation.2 | async-start | bytes 10485760 | tf_op jit(solution)/shard_map/all_gather | solution.py:336
  11.1 161.5 %all-to-all-start = ((s32[64,1,1]{2,1,0:T(1,128)}), s32[64,1,1]{2,1,0:T(1,128)S(1)}, u32[]{:S(2)}, u32[]{:S(2)}) async-start(s32[64,1,1]{2,1,0:T(1,128)} %copy.36), calls=%async_computation | async-start | bytes 65536 | tf_op jit(solution)/shard_map/all_to_all | solution.py:341
  111.3 20.0 %slice-start = ((s8[5242880]{0:T(1024)(128)(4,1)}), s8[1048576]{0:T(1024)(128)(4,1)S(1)}, s32[]{:S(2)}) async-start(s8[5242880]{0:T(1024)(128)(4,1)} %bitcast.33), calls=%async_computation.3 | async-start | bytes 2097152
  119.0 12.4 %slice-start.1 = ((s8[5242880]{0:T(1024)(128)(4,1)}), s8[4194304]{0:T(1024)(128)(4,1)S(1)}, s32[]{:S(2)}) async-start(s8[5242880]{0:T(1024)(128)(4,1)} %bitcast.33), calls=%async_computation.4 | async-start | bytes 8388608
  172.6 195.5 %all-to-all-start.1 = ((bf16[64,1,128,512]{3,2,1,0:T(8,128)(2,1)}), bf16[64,1,128,512]{3,2,1,0:T(8,128)(2,1)}, u32[]{:S(2)}, u32[]{:S(2)}) async-start(bf16[64,1,128,512]{3,2,1,0:T(8,128)(2,1)} %bitcast.32), calls=%async_computation.1 | async-start | bytes 16777216 | tf_op jit(solution)/shard_map/all_to_all | solution.py:340
  183.5 196.9 %copy-start = (f32[4,128,512]{2,1,0:T(8,128)S(1)}, f32[4,128,512]{2,1,0:T(8,128)}, u32[]{:S(2)}) copy-start(f32[4,128,512]{2,1,0:T(8,128)} %param.11) | copy-start | bytes 3145732
Sparse Core Ops, SparseCore 0:
  9.1 88.4 all-gather.1
where the time goes:
time: 391 us; the launch traced here: 389 us
  waiting for transfers between devices  252 us (64%)
  local copies, waits for them, and re-layouts  66.4 us (17%)
  starting transfers between devices  22.8 us (6%)
  matrix products  22.8 us (6%)
  between operations  14.1 us (4%)
  other arithmetic  10.9 us (3%)
    all_to_all x1, waiting for transfers between devices, per_device(): lax.all_to_all(buffer, 'col', split_axis=0, concat_axis=0, tiled=True)  183 us
    all_gather x1, waiting for transfers between devices, per_device(): lax.all_gather(panels, 'grp', axis=2, tiled=True)  67.5 us
    gather x4, local copies, waits for them, and re-layouts, pair_products(): right_rows = piece_rows[:, lower_table]  33.6 us
    scatter x1, local copies, waits for them, and re-layouts, pack_updates(): buffer = jnp.zeros((peer_count * capacity,) + picked.shape[1:], picked.dt...  14.1 us
    dot_general x1, matrix products, assemble(): jnp.einsum('tn,nrc->trc', select, arrived, preferred_element_type=jnp.flo...  12.3 us
    all_to_all x1, starting transfers between devices, per_device(): lax.all_to_all(routed, 'col', split_axis=0, concat_axis=0, tiled=True)  11.9 us
    all_to_all x1, starting transfers between devices, per_device(): lax.all_to_all(buffer, 'col', split_axis=0, concat_axis=0, tiled=True)  10.9 us
    dot_general x1, matrix products, pair_products(): jnp.einsum('fprw,fpcw->fprc', left_rows, right_rows, preferred_element_ty...  10.5 us
  transfers between devices with their start and end apart: 3, of which 2 were waited for; matrix products, arithmetic and copies ran while one was open for 22% of the time, Pallas kernels for 0%

commit v1 on v0

v1 whole, which is shorter than its diff:
```python
import functools

import jax
import jax.numpy as jnp
from jax import lax
from jax.experimental import pallas as pl
from jax.experimental.pallas import tpu as pltpu
from jax.sharding import PartitionSpec as P

MESH = pl.DeviceIdType.MESH

KINDS = "AEEAEEAE"
HALF = 32
UNIT = 2 * HALF
UP, DOWN = 0, 1
RING_X, RING_Z = 4, 8


def plan(kinds):
    ready = [0, 1, 14, 25.5, 37, 48, 48.5, 49]
    steps, x_free = [], 0.0
    for u, kind in enumerate(kinds):
        made = ready[u] + 1.5
        steps.append((ready[u], u, "make"))
        x_free = max(x_free, made) + 6.0
        at = x_free + 1.0
        if kind == "A":
            steps.append((at, u, "pass"))
            x_free += 6.0
            at = x_free + 1.0
        gap = 3.0
        for s in range(5):
            steps.append((at + gap * s, u, s))
        at += gap * 5
        if kind == "E":
            steps.append((at, u, "join"))
    steps.sort(key=lambda step: step[0])
    return [(u, what) for _, u, what in steps]


def kernel(
    kinds, chosen, label, own, parent, out,
    from_up, from_dn, lab_in, weight, product, xs, xr, ps, pr, fs, fr, zs, zr, ks, kr, summed,
    y_send, y_recv, l_send, l_recv, x_send, x_recv, p_send, p_recv, z_send, z_recv,
    k_send, k_recv,
):
    fronts, blocks, quarter, width = own.shape
    targets = parent.shape[0]
    units = len(kinds)
    chunks = quarter // HALF
    g, c = lax.axis_index("grp"), lax.axis_index("col")
    x, z, k = c // (2 * RING_Z), (c // 2) % RING_Z, c % 2
    pair = [x + 1 - 2 * (x % 2), 3 - x]
    across = (x + 2) % RING_X

    def device(xx, zz, kk):
        return {"grp": g, "col": xx * (2 * RING_Z) + zz * 2 + kk}

    to_core = device(x, z, 1 - k)
    to_pair = [[device(pair[v], z, k), device(pair[v], z, 1 - k)] for v in range(2)]
    to_z = [device(x, (z + 1) % RING_Z, k), device(x, (z + RING_Z - 1) % RING_Z, k)]
    to_y = [{"grp": (g + 1) % 4, "col": c}, {"grp": (g + 3) % 4, "col": c}]

    barrier = pltpu.get_barrier_semaphore()
    peers = [to_core] + to_pair[0] + to_pair[1] + to_z + to_y
    for peer in peers:
        pl.semaphore_signal(barrier, inc=1, device_id=peer, device_id_type=MESH)
    pl.semaphore_wait(barrier, len(peers))

    def remote(src, dst, send, recv, where):
        return pltpu.make_async_remote_copy(
            src_ref=src, dst_ref=dst, send_sem=send, recv_sem=recv,
            device_id=where, device_id_type=MESH,
        )

    y_copy = []
    for i in range(chunks):
        at = pl.ds(i * HALF, HALF)
        y_copy.append([
            remote(own.at[:, :, at], from_dn.at[i], y_send.at[i, 0], y_recv.at[i, 0], to_y[UP]),
            remote(own.at[:, :, at], from_up.at[i], y_send.at[i, 1], y_recv.at[i, 1], to_y[DOWN]),
        ])
    l_copy = [
        remote(label, lab_in.at[i], l_send.at[i], l_recv.at[i], where)
        for i, where in enumerate([to_core] + to_pair[0] + to_pair[1])
    ]
    for copy in l_copy:
        copy.start()
    for row in y_copy:
        for copy in row:
            copy.start()

    x_copy = [
        [
            [
                remote(
                    xs.at[u, v, d], xr.at[u, v, d + 1], x_send.at[u, v, d], x_recv.at[u, v, d],
                    ([to_core] + to_pair[v])[d],
                )
                for d in range(3)
            ]
            for v in range(2)
        ]
        for u in range(units)
    ]
    rank = [kinds[:u].count(kinds[u]) for u in range(units)]
    p_copy = []
    for u in range(units):
        src, dst = (ps, pr) if kinds[u] == "A" else (fs, fr)
        p_copy.append([
            remote(
                src.at[rank[u], v], dst.at[rank[u], v], p_send.at[u, v], p_recv.at[u, v],
                to_pair[1 - v][0],
            )
            for v in range(2)
        ])
    z_copy = []
    for u in range(units):
        row = []
        for way in range(2):
            hops = []
            for d in range(1, 5):
                at = (way, d - 1) if d < 4 else (way, d - 1, way)
                hops.append(remote(
                    zs[u].at[at], zr[u].at[at], z_send.at[u, way, d - 1],
                    z_recv.at[u, way, d - 1], to_z[way],
                ))
            row.append(hops)
        z_copy.append(row)
    k_copy = [
        remote(ks.at[i], kr.at[i], k_send.at[i], k_recv.at[i], to_y[UP]) for i in range(2)
    ]

    def row_of(u, v):
        if u < 2:
            return u * UNIT + v * HALF
        if u < 2 + chunks:
            return quarter * (1 + v) + (u - 2) * HALF
        return 3 * quarter + (u - 2 - chunks) * UNIT + v * HALF

    def owner(column, r):
        return column * (2 * RING_Z) + ((z + r) % RING_Z) * 2

    def make(u):
        if 2 <= u < 2 + chunks:
            for copy in y_copy[u - 2]:
                copy.wait_recv()

        def front(f, carry):
            def rows_of(b):
                if u < 2:
                    return [own[f, b, u * UNIT:(u + 1) * UNIT, :]]
                if u < 2 + chunks:
                    return [from_up[u - 2, f, b], from_dn[u - 2, f, b]]
                first = 2 * (u - 2 - chunks)
                return [from_dn[first, f, b], from_dn[first + 1, f, b]]

            def lanes_of(a):
                if u < 2 + chunks:
                    return [own[f, a]]
                return [from_up[i, f, a] for i in range(chunks)]

            for half in range(blocks // 2):
                top = 2 * (half + 1)
                left = jnp.concatenate([part for b in range(top) for part in rows_of(b)], axis=0)
                right = jnp.concatenate(
                    [part for a in (2 * half, 2 * half + 1) for part in lanes_of(a)], axis=0
                )
                made = lax.dot_general(
                    left, right, (((1,), (1,)), ((), ())), preferred_element_type=jnp.float32
                ).astype(jnp.bfloat16)
                for i in range(2):
                    a = 2 * half + i
                    for b in range(a + 1):
                        product[(f * blocks + a) * blocks + b] = made[
                            b * UNIT:(b + 1) * UNIT, i * quarter:(i + 1) * quarter
                        ]
            return carry

        lax.fori_loop(0, fronts, front, 0)

        def pack(j, carry):
            column, r = j // RING_Z, j % RING_Z
            for v in range(2):
                here = owner(x + column * (pair[1 - v] - x), r)
                there = owner(pair[v] + column * (across - pair[v]), r)
                rows = slice(v * HALF, (v + 1) * HALF)
                xr[u, v, 0, j] = product[chosen[0, here + k], rows, :]
                xs[u, v, 0, j] = product[chosen[0, here + 1 - k], rows, :]
                xs[u, v, 1, j] = product[chosen[0, there + k], rows, :]
                xs[u, v, 2, j] = product[chosen[0, there + 1 - k], rows, :]
            return carry

        lax.fori_loop(0, 2 * RING_Z, pack, 0)
        for v in range(2):
            for d in (1, 2, 0):
                x_copy[u][v][d].start()

    def weigh():
        for copy in l_copy:
            copy.wait_recv()

        def slot(j, carry):
            column, r = j // RING_Z, j % RING_Z
            for v in range(2):
                at = owner(x + column * (pair[1 - v] - x), r) + k
                rows = [
                    label[pl.ds(at, 1), :], lab_in[0, pl.ds(at, 1), :],
                    lab_in[1 + 2 * v, pl.ds(at, 1), :], lab_in[2 + 2 * v, pl.ds(at, 1), :],
                ]
                for s in range(4):
                    full = jnp.broadcast_to(rows[s], (8, 128))
                    for t in range(targets):
                        weight[v, s, j, t] = jnp.where(full == t + 1, 1.0, 0.0).astype(jnp.float32)
            return carry

        lax.fori_loop(0, 2 * RING_Z, slot, 0)

    tile = (HALF // 8, 8, 128)

    def widen(value):
        return value.astype(jnp.float32).reshape(tile)

    def narrow(value):
        return value.reshape(HALF, 128).astype(jnp.bfloat16)

    def near(u, v, j):
        total = [None] * targets
        for s in range(4):
            block = widen(xr[u, v, s, j])
            for t in range(targets):
                part = block * weight[v, s, j, t][None]
                total[t] = part if s == 0 else total[t] + part
        return total

    def both(u, v, column, r):
        total = near(u, v, column * RING_Z + r)
        if kinds[u] == "A":
            total = [total[t] + widen(pr[rank[u], v, r, t]) for t in range(targets)]
        return total

    columns = {"A": 1, "E": 2}

    def wait_x(u):
        for v in range(2):
            for copy in x_copy[u][v]:
                copy.wait_recv()

    def pass_on(u):
        wait_x(u)

        for v in range(2):
            def slot(r, carry):
                total = near(u, v, RING_Z + r)
                for t in range(targets):
                    ps[rank[u], v, r, t] = narrow(total[t])
                return carry

            lax.fori_loop(0, RING_Z, slot, 0)
            p_copy[u][v].start()

    def hop(u, step):
        d = 4 - step
        wide = columns[kinds[u]]
        if step == 0:
            if kinds[u] == "A":
                for copy in p_copy[u]:
                    copy.wait_recv()
            else:
                wait_x(u)
        for way in range(2):
            r = d if way == UP else RING_Z - d
            if step > 0:
                z_copy[u][way][d].wait_recv()

            def add(v, column, arrived):
                total = both(u, v, column, r)
                for t in range(targets):
                    value = total[t]
                    if arrived:
                        value = value + widen(zr[u][way, d, v, column, t])
                    zs[u][way, d - 1, v, column, t] = narrow(value)

            if d >= 3:
                for v in range(2):
                    if d == 4 and v != way:
                        continue

                    def body(column, carry):
                        add(v, column, d == 3 and v == way)
                        return carry

                    lax.fori_loop(0, wide, body, 0)
            else:
                def body(j, carry):
                    add(j // wide, j % wide, True)
                    return carry

                lax.fori_loop(0, 2 * wide, body, 0)
            z_copy[u][way][d - 1].start()

    def settle(u, v, total):
        back = u - 2 - chunks
        for t in range(targets):
            if back >= 0:
                ks[back, t, v * HALF:(v + 1) * HALF] = narrow(total[t])
            else:
                row = row_of(u, v)
                summed[t, row:row + HALF] = total[t].reshape(HALF, 128)

    done = []

    def finished(u):
        done.append(u)
        if u >= 2 + chunks:
            k_copy[u - 2 - chunks].start()
        if sorted(done)[:2] == [0, 1] and u < 2:
            write(0)
        if u >= 2 and u < 2 + chunks and all(2 + i in done for i in range(chunks)):
            write(1)
            write(2)

    def end(u):
        for way in range(2):
            z_copy[u][way][0].wait_recv()
        for v in range(2):
            for column in reversed(range(columns[kinds[u]])):
                total = both(u, v, column, 0)
                total = [
                    total[t] + widen(zr[u][UP, 0, v, column, t])
                    + widen(zr[u][DOWN, 0, v, column, t])
                    for t in range(targets)
                ]
                if column == 1:
                    for t in range(targets):
                        fs[rank[u], v, t] = narrow(total[t])
                    p_copy[u][v].start()
                elif kinds[u] == "A":
                    settle(u, v, total)
                else:
                    row = row_of(u, v)
                    for t in range(targets):
                        summed[t, row:row + HALF] = total[t].reshape(HALF, 128)
        if kinds[u] == "A":
            finished(u)

    def join(u):
        for v in range(2):
            p_copy[u][v].wait_recv()
            row = row_of(u, v)
            total = [
                summed[t, row:row + HALF].reshape(tile) + widen(fr[rank[u], v, t])
                for t in range(targets)
            ]
            settle(u, v, total)
        finished(u)

    member = [g, (g + 1) % 4, (g + 3) % 4, (g + 2) % 4]

    def write(piece):
        at = pl.ds(pl.multiple_of(member[piece] * quarter, quarter), quarter)
        for t in range(targets):
            if piece == 3:
                total = jnp.concatenate(
                    [kr[i, t].astype(jnp.float32) for i in range(2)], axis=0
                )
            else:
                total = summed[t, piece * quarter:(piece + 1) * quarter]
            out[t, :, at] = parent[t, :, at] - total.T

    weighed = False
    for u, what in plan(kinds):
        if what == "make":
            make(u)
            continue
        if not weighed:
            weigh()
            weighed = True
        if what == "pass":
            pass_on(u)
        elif what == "join":
            join(u)
        elif what == 4:
            end(u)
        else:
            hop(u, what)
    for copy in k_copy:
        copy.wait_recv()
    write(3)
    for row in y_copy + p_copy:
        for copy in row:
            copy.wait_send()
    for copy in l_copy + k_copy:
        copy.wait_send()
    for u in range(units):
        for row in x_copy[u] + z_copy[u]:
            for copy in row:
                copy.wait_send()


def assemble(chosen, label, panels, parent):
    fronts, blocks, quarter, width = panels.shape
    targets = parent.shape[0]
    kinds = KINDS
    units = len(kinds)
    chunks = quarter // HALF
    bf16, f32 = jnp.bfloat16, jnp.float32
    dma = pltpu.SemaphoreType.DMA
    vmem = pltpu.VMEM
    hops = [
        vmem((2, 4, 2, 1 if kind == "A" else 2, targets, HALF, quarter), bf16) for kind in kinds
    ]
    passed = vmem((max(1, kinds.count("A")), 2, RING_Z, targets, HALF, quarter), bf16)
    joined = vmem((max(1, kinds.count("E")), 2, targets, HALF, quarter), bf16)
    gathered = vmem((chunks, fronts, blocks, HALF, width), bf16)
    arrays = pl.BlockSpec(memory_space=vmem)
    return pl.pallas_call(
        functools.partial(kernel, kinds),
        out_shape=jax.ShapeDtypeStruct(parent.shape, parent.dtype),
        in_specs=[pl.BlockSpec(memory_space=pltpu.SMEM), arrays, arrays, arrays],
        out_specs=arrays,
        scratch_shapes=[
            gathered, gathered,
            vmem((5,) + label.shape, jnp.int32),
            vmem((2, 4, 2 * RING_Z, targets, 8, 128), f32),
            vmem((fronts * blocks * blocks, UNIT, quarter), bf16),
            vmem((units, 2, 3, 2 * RING_Z, HALF, quarter), bf16),
            vmem((units, 2, 4, 2 * RING_Z, HALF, quarter), bf16),
            passed, passed, joined, joined, hops, hops,
            vmem((2, targets, UNIT, quarter), bf16), vmem((2, targets, UNIT, quarter), bf16),
            vmem((targets, 4 * quarter, quarter), f32),
            dma((chunks, 2)), dma((chunks, 2)), dma((5,)), dma((5,)),
            dma((units, 2, 3)), dma((units, 2, 3)), dma((units, 2)), dma((units, 2)),
            dma((units, 2, 4)), dma((units, 2, 4)), dma((2,)), dma((2,)),
        ],
        compiler_params=pltpu.CompilerParams(
            collective_id=0, has_side_effects=True, vmem_limit_bytes=63 * 1024 * 1024
        ),
    )(chosen, label, panels, parent)


def per_device(panels, parent, src_block, dest_owner, target, counts):
    blocks = panels.shape[1]
    pairs = blocks * (blocks + 1) // 2
    peers = lax.axis_size("col")
    slots = src_block.shape[1]
    named = dest_owner.reshape(1, slots) == jnp.arange(peers, dtype=jnp.int32)[:, None]
    within = src_block % pairs
    upper = sum((within >= a * (a + 1) // 2).astype(jnp.int32) for a in range(1, blocks))
    lower = within - upper * (upper + 1) // 2
    code = (src_block // pairs * blocks + upper) * blocks + lower
    chosen = jnp.sum(jnp.where(named, code, 0), axis=1)
    live = jnp.arange(slots, dtype=jnp.int32) < counts[0]
    mark = jnp.where(live, target + 1, 0).reshape(1, slots)
    label = jnp.sum(jnp.where(named, mark, 0), axis=1)
    return assemble(
        chosen.reshape(1, peers), jnp.broadcast_to(label[:, None], (peers, 128)), panels, parent
    )


def solution(mesh):
    placed = (
        P("col", None, "grp", None),
        P("col", "grp", None),
        P("col", None),
        P("col", None),
        P("col"),
        P("col"),
    )
    return jax.shard_map(
        per_device, mesh=mesh, in_specs=placed, out_specs=P("col", "grp", None), check_vma=False
    )
```

time: 391 us -> 160 us (0.41)
  waiting for transfers between devices: 252 us -> 0 us
  Pallas kernels: 0 us -> 153 us
  local copies, waits for them, and re-layouts: 66.4 us -> 2.95 us
  matrix products: 22.8 us -> 0 us
  starting transfers between devices: 22.8 us -> 0 us
  between operations: 14.1 us -> 0.66 us
  other arithmetic: 10.9 us -> 2.68 us
    all_to_all x2 -> x0, waiting for transfers between devices: 183 us -> none  [the longest x1 183 us: per_device(): lax.all_to_all(buffer, 'col', split_axis=0, concat_axis=0, tiled=True)]
    pallas_call x0 -> x1, Pallas kernels: none -> 153 us  [assemble(): pl.pallas_call(functools.partial(kernel, kinds), out_shape=jax.ShapeDtype...]
    all_gather x1 -> x0, waiting for transfers between devices: 67.5 us -> none  [per_device(): lax.all_gather(panels, 'grp', axis=2, tiled=True)]
    gather x6 -> x0, local copies, waits for them, and re-layouts: 46.5 us -> none  [the longest x4 33.6 us: pair_products(): right_rows = piece_rows[:, lower_table]]
    all_to_all x2 -> x0, starting transfers between devices: 22.8 us -> none  [the longest x1 11.9 us: per_device(): lax.all_to_all(routed, 'col', split_axis=0, concat_axis=0, tiled=True)]
    dot_general x2 -> x0, matrix products: 22.8 us -> none  [the longest x1 12.3 us: assemble(): jnp.einsum('tn,nrc->trc', select, arrived, preferred_element_type=jnp.flo...]
    scatter x2 -> x0, local copies, waits for them, and re-layouts: 14.9 us -> none  [the longest x1 14.1 us: pack_updates(): buffer = jnp.zeros((peer_count * capacity,) + picked.shape[1:], picked.dt...]
    select_n x3 -> x1, other arithmetic: 5.95 us -> 0.66 us  [per_device(): mark = jnp.where(live, target + 1, 0).reshape(1, slots)]
  transfers between devices with their start and end apart: 3 -> 0, of which waited for: 2 -> 0; matrix products, arithmetic and copies ran while one was open for 22% -> 0% of each run, Pallas kernels for 0% -> 0%
where the time goes in v1:
time: 160 us
  Pallas kernels  153 us (96%)
  local copies, waits for them, and re-layouts  2.95 us (2%)
  other arithmetic  2.68 us (2%)
    pallas_call x1, Pallas kernels, assemble(): pl.pallas_call(functools.partial(kernel, kinds), out_shape=jax.ShapeDtype...  153 us

profile of v1, /device:TPU:8, one launch (start us, length us, event | category | flops | bytes accessed | tf_op | source)
XLA Modules:
  0.0 159.7 jit_solution(14530191307269439571)
XLA Ops:
  0.7 0.7 compare_select_fusion
  1.3 0.7 add_bitcast_fusion
  2.0 1.3 select_reduce_fusion
  3.3 0.7 broadcast_in_dim.36.label
  4.0 153.4 %shard_map.64 = f32[4,128,512]{2,1,0:T(8,128)} custom-call(s32[1,64]{1,0:T(1,128)} %bitcast.6, s32[64,128]{1,0:T(8,128)} %broadcast_in_dim.36.label, bf16[4,4,128,512]{3,2,1,0:T(8,128)(2,1)} %own.1, f32[4,128,512]{2,1,0:T(8,128)} %parent.1), custom_call_target="tpu_custom_call" | custom-call | tf_op jit(solution)/shard_map/pallas_call | solution.py:417
  157.5 2.3 %copy.9 = f32[4,128,512]{2,1,0:T(8,128)} copy(f32[4,128,512]{2,1,0:T(8,128)} %shard_map.64) | data formatting | bytes 2097152

commit v2 on v1

--- a/solution.py
+++ b/solution.py
@@ -9,49 +9,41 @@
 
 MESH = pl.DeviceIdType.MESH
 
-KINDS = "AEEAEEAE"
-HALF = 32
+KINDS = "EEEAEAEEEEAAEEAA"
+MAKE, PASS, JOIN = 5, 6, 7
+ORDER = [
+    5, 13, 0, 1, 8, 16, 2, 21, 9, 30, 17, 3, 10, 32, 18, 4,
+    46, 11, 33, 29, 24, 19, 61, 40, 25, 34, 12, 53, 48, 41, 26, 7,
+    20, 35, 56, 49, 42, 27, 69, 15, 57, 104, 36, 37, 96, 50, 43, 23,
+    28, 58, 105, 118, 97, 39, 51, 44, 64, 59, 77, 106, 72, 45, 98, 52,
+    65, 112, 60, 107, 126, 73, 99, 86, 66, 113, 108, 94, 55, 63, 74, 100,
+    120, 67, 114, 75, 121, 80, 111, 68, 115, 88, 76, 103, 71, 122, 81, 116,
+    89, 79, 123, 82, 90, 124, 83, 91, 84, 92,
+]
+HALF = 16
 UNIT = 2 * HALF
 UP, DOWN = 0, 1
 RING_X, RING_Z = 4, 8
 
 
-def plan(kinds):
-    ready = [0, 1, 14, 25.5, 37, 48, 48.5, 49]
-    steps, x_free = [], 0.0
-    for u, kind in enumerate(kinds):
-        made = ready[u] + 1.5
-        steps.append((ready[u], u, "make"))
-        x_free = max(x_free, made) + 6.0
-        at = x_free + 1.0
-        if kind == "A":
-            steps.append((at, u, "pass"))
-            x_free += 6.0
-            at = x_free + 1.0
-        gap = 3.0
-        for s in range(5):
-            steps.append((at + gap * s, u, s))
-        at += gap * 5
-        if kind == "E":
-            steps.append((at, u, "join"))
-    steps.sort(key=lambda step: step[0])
-    return [(u, what) for _, u, what in steps]
-
-
 def kernel(
-    kinds, chosen, label, own, parent, out,
-    from_up, from_dn, lab_in, weight, product, xs, xr, ps, pr, fs, fr, zs, zr, ks, kr, summed,
-    y_send, y_recv, l_send, l_recv, x_send, x_recv, p_send, p_recv, z_send, z_recv,
+    kinds, chosen, label, panels, out,
+    own, from_up, from_dn, lab_in, weight, product, xs, xr, ps, pr, fs, fr, zs, zr, ks, kr,
+    summed,
+    own_sem, y_send, y_recv, l_send, l_recv, x_send, x_recv, p_send, p_recv, z_send, z_recv,
     k_send, k_recv,
 ):
     fronts, blocks, quarter, width = own.shape
-    targets = parent.shape[0]
+    targets = out.shape[0]
     units = len(kinds)
-    chunks = quarter // HALF
+    chunks = quarter // UNIT
     g, c = lax.axis_index("grp"), lax.axis_index("col")
     x, z, k = c // (2 * RING_Z), (c // 2) % RING_Z, c % 2
     pair = [x + 1 - 2 * (x % 2), 3 - x]
     across = (x + 2) % RING_X
+
+    load = pltpu.make_async_copy(panels, own, own_sem)
+    load.start()
 
     def device(xx, zz, kk):
         return {"grp": g, "col": xx * (2 * RING_Z) + zz * 2 + kk}
@@ -73,12 +65,20 @@
             device_id=where, device_id_type=MESH,
         )
 
+    def dn_row(i):
+        return (i + chunks // 2) % chunks * UNIT
+
     y_copy = []
     for i in range(chunks):
-        at = pl.ds(i * HALF, HALF)
+        up_at, dn_at = pl.ds(dn_row(i), UNIT), pl.ds(i * UNIT, UNIT)
         y_copy.append([
-            remote(own.at[:, :, at], from_dn.at[i], y_send.at[i, 0], y_recv.at[i, 0], to_y[UP]),
-            remote(own.at[:, :, at], from_up.at[i], y_send.at[i, 1], y_recv.at[i, 1], to_y[DOWN]),
+            remote(
+                own.at[:, :, up_at], from_dn.at[i], y_send.at[i, UP], y_recv.at[i, UP], to_y[UP]
+            ),
+            remote(
+                own.at[:, :, dn_at], from_up.at[i], y_send.at[i, DOWN], y_recv.at[i, DOWN],
+                to_y[DOWN],
+            ),
         ])
     l_copy = [
         remote(label, lab_in.at[i], l_send.at[i], l_recv.at[i], where)
@@ -86,6 +86,7 @@
     ]
     for copy in l_copy:
         copy.start()
+    load.wait()
     for row in y_copy:
         for copy in row:
             copy.start()
@@ -128,37 +129,47 @@
             row.append(hops)
         z_copy.append(row)
     k_copy = [
-        remote(ks.at[i], kr.at[i], k_send.at[i], k_recv.at[i], to_y[UP]) for i in range(2)
+        [
+            remote(ks.at[i], kr.at[way, i], k_send.at[i, way], k_recv.at[i, way], to_y[way])
+            for way in range(2)
+        ]
+        for i in range(chunks)
     ]
 
-    def row_of(u, v):
-        if u < 2:
-            return u * UNIT + v * HALF
-        if u < 2 + chunks:
-            return quarter * (1 + v) + (u - 2) * HALF
-        return 3 * quarter + (u - 2 - chunks) * UNIT + v * HALF
+    def row_of(u):
+        if u < chunks:
+            return u * UNIT
+        chunk, side = (u - chunks) // 2, (u - chunks) % 2
+        return quarter + chunk * UNIT if side == 0 else 2 * quarter + dn_row(chunk)
 
     def owner(column, r):
         return column * (2 * RING_Z) + ((z + r) % RING_Z) * 2
 
-    def make(u):
-        if 2 <= u < 2 + chunks:
-            for copy in y_copy[u - 2]:
-                copy.wait_recv()
+    arrived = set()
+
+    def make(group):
+        chunk = group - 2 if group < 2 + chunks else group - 2 - chunks
+        own_rows, meeting = group < 2, group >= 2 + chunks
+        if not own_rows:
+            for i in range(max(chunk, chunks // 2 - 1 if meeting else 0) + 1):
+                if i not in arrived:
+                    arrived.add(i)
+                    for copy in y_copy[i]:
+                        copy.wait_recv()
 
         def front(f, carry):
             def rows_of(b):
-                if u < 2:
-                    return [own[f, b, u * UNIT:(u + 1) * UNIT, :]]
-                if u < 2 + chunks:
-                    return [from_up[u - 2, f, b], from_dn[u - 2, f, b]]
-                first = 2 * (u - 2 - chunks)
-                return [from_dn[first, f, b], from_dn[first + 1, f, b]]
+                if own_rows:
+                    return [own[f, b, group * 2 * UNIT:(group + 1) * 2 * UNIT, :]]
+                if meeting:
+                    return [from_dn[chunk, f, b], from_up[chunk, f, b]]
+                return [from_up[chunk, f, b], from_dn[chunk, f, b]]
 
             def lanes_of(a):
-                if u < 2 + chunks:
+                if not meeting:
                     return [own[f, a]]
-                return [from_up[i, f, a] for i in range(chunks)]
+                half = range(chunks // 2)
+                return [from_up[i, f, a] for i in half] + [from_dn[i, f, a] for i in half]
 
             for half in range(blocks // 2):
                 top = 2 * (half + 1)
@@ -168,30 +179,46 @@
                 )
                 made = lax.dot_general(
                     left, right, (((1,), (1,)), ((), ())), preferred_element_type=jnp.float32
-                ).astype(jnp.bfloat16)
+                )
                 for i in range(2):
                     a = 2 * half + i
                     for b in range(a + 1):
-                        product[(f * blocks + a) * blocks + b] = made[
-                            b * UNIT:(b + 1) * UNIT, i * quarter:(i + 1) * quarter
-                        ]
+                        at = 2 * b * UNIT
+                        lanes = slice(i * quarter, (i + 1) * quarter)
+                        if meeting:
+                            first = lax.broadcasted_iota(
+                                jnp.int32, (UNIT, quarter), 1
+                            ) < quarter // 2
+                            product[(f * blocks + a) * blocks + b, :UNIT] = jnp.where(
+                                first, made[at:at + UNIT, lanes], made[at + UNIT:at + 2 * UNIT, lanes]
+                            ).astype(jnp.bfloat16)
+                        else:
+                            product[(f * blocks + a) * blocks + b] = made[
+                                at:at + 2 * UNIT, lanes
+                            ].astype(jnp.bfloat16)
             return carry
 
         lax.fori_loop(0, fronts, front, 0)
-
-        def pack(j, carry):
+        if meeting:
+            pack(3 * chunks + chunk, 0)
+        else:
+            pack(2 * group, 0)
+            pack(2 * group + 1, UNIT)
+
+    def pack(u, first):
+        def slot(j, carry):
             column, r = j // RING_Z, j % RING_Z
             for v in range(2):
                 here = owner(x + column * (pair[1 - v] - x), r)
                 there = owner(pair[v] + column * (across - pair[v]), r)
-                rows = slice(v * HALF, (v + 1) * HALF)
+                rows = slice(first + v * HALF, first + (v + 1) * HALF)
                 xr[u, v, 0, j] = product[chosen[0, here + k], rows, :]
                 xs[u, v, 0, j] = product[chosen[0, here + 1 - k], rows, :]
                 xs[u, v, 1, j] = product[chosen[0, there + k], rows, :]
                 xs[u, v, 2, j] = product[chosen[0, there + 1 - k], rows, :]
             return carry
 
-        lax.fori_loop(0, 2 * RING_Z, pack, 0)
+        lax.fori_loop(0, 2 * RING_Z, slot, 0)
         for v in range(2):
             for d in (1, 2, 0):
                 x_copy[u][v][d].start()
@@ -273,11 +300,11 @@
             if step > 0:
                 z_copy[u][way][d].wait_recv()
 
-            def add(v, column, arrived):
+            def add(v, column, more):
                 total = both(u, v, column, r)
                 for t in range(targets):
                     value = total[t]
-                    if arrived:
+                    if more:
                         value = value + widen(zr[u][way, d, v, column, t])
                     zs[u][way, d - 1, v, column, t] = narrow(value)
 
@@ -300,31 +327,34 @@
             z_copy[u][way][d - 1].start()
 
     def settle(u, v, total):
-        back = u - 2 - chunks
         for t in range(targets):
-            if back >= 0:
-                ks[back, t, v * HALF:(v + 1) * HALF] = narrow(total[t])
+            value = total[t].reshape(HALF, 128)
+            if u >= 3 * chunks:
+                ks[u - 3 * chunks, t, v * HALF:(v + 1) * HALF] = value.astype(jnp.bfloat16)
             else:
-                row = row_of(u, v)
-                summed[t, row:row + HALF] = total[t].reshape(HALF, 128)
+                row = row_of(u) + v * HALF
+                summed[t, row:row + HALF] = value
 
     done = []
 
     def finished(u):
         done.append(u)
-        if u >= 2 + chunks:
-            k_copy[u - 2 - chunks].start()
-        if sorted(done)[:2] == [0, 1] and u < 2:
-            write(0)
-        if u >= 2 and u < 2 + chunks and all(2 + i in done for i in range(chunks)):
-            write(1)
-            write(2)
+        if u >= 3 * chunks:
+            for copy in k_copy[u - 3 * chunks]:
+                copy.start()
+        for piece in range(3):
+            if piece == 0:
+                members = list(range(chunks))
+            else:
+                members = list(range(chunks + piece - 1, 3 * chunks, 2))
+            if u in members and all(i in done for i in members):
+                write(piece)
 
     def end(u):
         for way in range(2):
             z_copy[u][way][0].wait_recv()
-        for v in range(2):
-            for column in reversed(range(columns[kinds[u]])):
+        for column in reversed(range(columns[kinds[u]])):
+            for v in range(2):
                 total = both(u, v, column, 0)
                 total = [
                     total[t] + widen(zr[u][UP, 0, v, column, t])
@@ -338,21 +368,24 @@
                 elif kinds[u] == "A":
                     settle(u, v, total)
                 else:
-                    row = row_of(u, v)
                     for t in range(targets):
-                        summed[t, row:row + HALF] = total[t].reshape(HALF, 128)
+                        summed[t, row_held(u) + v * HALF:row_held(u) + (v + 1) * HALF] = total[
+                            t
+                        ].reshape(HALF, 128)
         if kinds[u] == "A":
             finished(u)
+
+    def row_held(u):
+        return row_of(u) if u < 3 * chunks else 3 * quarter + (u - 3 * chunks) * UNIT
 
     def join(u):
         for v in range(2):
             p_copy[u][v].wait_recv()
-            row = row_of(u, v)
-            total = [
+            row = row_held(u) + v * HALF
+            settle(u, v, [
                 summed[t, row:row + HALF].reshape(tile) + widen(fr[rank[u], v, t])
                 for t in range(targets)
-            ]
-            settle(u, v, total)
+            ])
         finished(u)
 
     member = [g, (g + 1) % 4, (g + 3) % 4, (g + 2) % 4]
@@ -361,36 +394,42 @@
         at = pl.ds(pl.multiple_of(member[piece] * quarter, quarter), quarter)
         for t in range(targets):
             if piece == 3:
-                total = jnp.concatenate(
-                    [kr[i, t].astype(jnp.float32) for i in range(2)], axis=0
+                order = [(i + chunks // 2) % chunks for i in range(chunks)]
+                below = jnp.concatenate([kr[UP, i, t].astype(jnp.float32) for i in order], axis=0)
+                above = jnp.concatenate(
+                    [kr[DOWN, i, t].astype(jnp.float32) for i in range(chunks)], axis=0
                 )
+                first = lax.broadcasted_iota(jnp.int32, (quarter, quarter), 1) < quarter // 2
+                total = jnp.where(first, below, above)
             else:
                 total = summed[t, piece * quarter:(piece + 1) * quarter]
-            out[t, :, at] = parent[t, :, at] - total.T
+            out[t, :, at] = total.T
 
     weighed = False
-    for u, what in plan(kinds):
-        if what == "make":
+    for item in ORDER:
+        u, what = item // 8, item % 8
+        if what == MAKE:
             make(u)
             continue
         if not weighed:
             weigh()
             weighed = True
-        if what == "pass":
+        if what == PASS:
             pass_on(u)
-        elif what == "join":
+        elif what == JOIN:
             join(u)
         elif what == 4:
             end(u)
         else:
             hop(u, what)
-    for copy in k_copy:
-        copy.wait_recv()
+    for row in k_copy:
+        for copy in row:
+            copy.wait_recv()
     write(3)
-    for row in y_copy + p_copy:
+    for row in y_copy + p_copy + k_copy:
         for copy in row:
             copy.wait_send()
-    for copy in l_copy + k_copy:
+    for copy in l_copy:
         copy.wait_send()
     for u in range(units):
         for row in x_copy[u] + z_copy[u]:
@@ -398,12 +437,11 @@
                 copy.wait_send()
 
 
-def assemble(chosen, label, panels, parent):
+def assemble(chosen, label, panels, targets):
     fronts, blocks, quarter, width = panels.shape
-    targets = parent.shape[0]
     kinds = KINDS
     units = len(kinds)
-    chunks = quarter // HALF
+    chunks = quarter // UNIT
     bf16, f32 = jnp.bfloat16, jnp.float32
     dma = pltpu.SemaphoreType.DMA
     vmem = pltpu.VMEM
@@ -412,31 +450,34 @@
     ]
     passed = vmem((max(1, kinds.count("A")), 2, RING_Z, targets, HALF, quarter), bf16)
     joined = vmem((max(1, kinds.count("E")), 2, targets, HALF, quarter), bf16)
-    gathered = vmem((chunks, fronts, blocks, HALF, width), bf16)
+    gathered = vmem((chunks, fronts, blocks, UNIT, width), bf16)
     arrays = pl.BlockSpec(memory_space=vmem)
     return pl.pallas_call(
         functools.partial(kernel, kinds),
-        out_shape=jax.ShapeDtypeStruct(parent.shape, parent.dtype),
-        in_specs=[pl.BlockSpec(memory_space=pltpu.SMEM), arrays, arrays, arrays],
+        out_shape=jax.ShapeDtypeStruct((targets, quarter, 4 * quarter), f32),
+        in_specs=[
+            pl.BlockSpec(memory_space=pltpu.SMEM), arrays, pl.BlockSpec(memory_space=pl.ANY)
+        ],
         out_specs=arrays,
         scratch_shapes=[
-            gathered, gathered,
+            vmem(panels.shape, bf16), gathered, gathered,
             vmem((5,) + label.shape, jnp.int32),
             vmem((2, 4, 2 * RING_Z, targets, 8, 128), f32),
-            vmem((fronts * blocks * blocks, UNIT, quarter), bf16),
+            vmem((fronts * blocks * blocks, 2 * UNIT, quarter), bf16),
             vmem((units, 2, 3, 2 * RING_Z, HALF, quarter), bf16),
             vmem((units, 2, 4, 2 * RING_Z, HALF, quarter), bf16),
             passed, passed, joined, joined, hops, hops,
-            vmem((2, targets, UNIT, quarter), bf16), vmem((2, targets, UNIT, quarter), bf16),
+            vmem((chunks, targets, UNIT, quarter), bf16),
+            vmem((2, chunks, targets, UNIT, quarter), bf16),
             vmem((targets, 4 * quarter, quarter), f32),
-            dma((chunks, 2)), dma((chunks, 2)), dma((5,)), dma((5,)),
+            dma, dma((chunks, 2)), dma((chunks, 2)), dma((5,)), dma((5,)),
             dma((units, 2, 3)), dma((units, 2, 3)), dma((units, 2)), dma((units, 2)),
-            dma((units, 2, 4)), dma((units, 2, 4)), dma((2,)), dma((2,)),
+            dma((units, 2, 4)), dma((units, 2, 4)), dma((chunks, 2)), dma((chunks, 2)),
         ],
         compiler_params=pltpu.CompilerParams(
             collective_id=0, has_side_effects=True, vmem_limit_bytes=63 * 1024 * 1024
         ),
-    )(chosen, label, panels, parent)
+    )(chosen, label, panels)
 
 
 def per_device(panels, parent, src_block, dest_owner, target, counts):
@@ -453,9 +494,11 @@
     live = jnp.arange(slots, dtype=jnp.int32) < counts[0]
     mark = jnp.where(live, target + 1, 0).reshape(1, slots)
     label = jnp.sum(jnp.where(named, mark, 0), axis=1)
-    return assemble(
-        chosen.reshape(1, peers), jnp.broadcast_to(label[:, None], (peers, 128)), panels, parent
+    total = assemble(
+        chosen.reshape(1, peers), jnp.broadcast_to(label[:, None], (peers, 128)), panels,
+        parent.shape[0],
     )
+    return parent - total
 
 
 def solution(mesh):

time: 160 us -> 109 us (0.68)
  Pallas kernels: 153 us -> 102 us
  other arithmetic: 2.68 us -> 5.4 us
  local copies, waits for them, and re-layouts: 2.95 us -> 0.69 us
    pallas_call x1, Pallas kernels: 153 us -> 102 us  [assemble(): pl.pallas_call(functools.partial(kernel, kinds), out_shape=jax.ShapeDtype...]
    sub x0 -> x1, other arithmetic: none -> 2.72 us  [per_device(): return parent - total]
    unnamed x1 -> x0, local copies, waits for them, and re-layouts: 2.26 us -> none
where the time goes in v2:
time: 109 us
  Pallas kernels  102 us (94%)
  other arithmetic  5.4 us (5%)
    pallas_call x1, Pallas kernels, assemble(): pl.pallas_call(functools.partial(kernel, kinds), out_shape=jax.ShapeDtype...  102 us
    sub x1, other arithmetic, per_device(): return parent - total  2.72 us

profile of v2, /device:TPU:8, one launch (start us, length us, event | category | flops | bytes accessed | tf_op | source)
XLA Modules:
  0.0 109.1 jit_solution(7175205349962462331)
XLA Ops:
  0.7 0.7 compare_select_fusion
  1.3 0.7 add_bitcast_fusion
  2.0 1.3 %select_reduce_fusion = (s32[64]{0:T(128)S(1)}, s32[64]{0:T(128)}) fusion(s32[40]{0:T(128)S(1)} %compare_select_fusion, s32[40]{0:T(128)} %bitcast.7, s32[40]{0:T(128)S(1)} %add_bitcast_fusion), kind=kLoop, calls=%fused_computation | loop fusion | flops 12672 | bytes 992 | tf_op jit(solution)/shard_map/reduce_sum | solution.py:496
  3.3 0.7 broadcast_in_dim.36.label
  4.0 102.3 %shard_map.64 = f32[4,128,512]{2,1,0:T(8,128)} custom-call(s32[1,64]{1,0:T(1,128)} %bitcast.6, s32[64,128]{1,0:T(8,128)} %broadcast_in_dim.36.label, bf16[4,4,128,512]{3,2,1,0:T(8,128)(2,1)} %panels.1), custom_call_target="tpu_custom_call" | custom-call | tf_op jit(solution)/shard_map/pallas_call | solution.py:455
  106.4 2.7 %sub.19 = f32[4,128,512]{2,1,0:T(8,128)} subtract(f32[4,128,512]{2,1,0:T(8,128)} %param.7, f32[4,128,512]{2,1,0:T(8,128)} %shard_map.64) | non-fusion elementwise | flops 262144 | bytes 3145728 | tf_op jit(solution)/shard_map/sub | solution.py:501

commit v3 on v2

--- a/solution.py
+++ b/solution.py
@@ -27,11 +27,11 @@
 
 
 def kernel(
-    kinds, chosen, label, panels, out,
-    own, from_up, from_dn, lab_in, weight, product, xs, xr, ps, pr, fs, fr, zs, zr, ks, kr,
-    summed,
-    own_sem, y_send, y_recv, l_send, l_recv, x_send, x_recv, p_send, p_recv, z_send, z_recv,
-    k_send, k_recv,
+    kinds, counts_in, src_block_in, owner_in, target_in, panels, out,
+    counts, src_block, owner_of, target, own, gathered, label, lab_in, row, chosen, weight, product, xs, xr, ps, pr, fs, fr,
+    z3s, z3r, z4s, z4r, ks, kr, summed,
+    list_sem, own_sem, row_sem, y_send, y_recv, l_send, l_recv, x_send, x_recv, p_send, p_recv,
+    z_send, z_recv, k_send, k_recv,
 ):
     fronts, blocks, quarter, width = own.shape
     targets = out.shape[0]
@@ -42,8 +42,16 @@
     pair = [x + 1 - 2 * (x % 2), 3 - x]
     across = (x + 2) % RING_X
 
+    lists = [
+        pltpu.make_async_copy(src, dst, list_sem.at[i])
+        for i, (src, dst) in enumerate([
+            (counts_in, counts), (src_block_in, src_block), (owner_in, owner_of),
+            (target_in, target),
+        ])
+    ]
     load = pltpu.make_async_copy(panels, own, own_sem)
-    load.start()
+    for copy in lists + [load]:
+        copy.start()
 
     def device(xx, zz, kk):
         return {"grp": g, "col": xx * (2 * RING_Z) + zz * 2 + kk}
@@ -57,7 +65,29 @@
     peers = [to_core] + to_pair[0] + to_pair[1] + to_z + to_y
     for peer in peers:
         pl.semaphore_signal(barrier, inc=1, device_id=peer, device_id_type=MESH)
-    pl.semaphore_wait(barrier, len(peers))
+
+    for copy in lists:
+        copy.wait()
+    slots, ranks = src_block.shape[1], label.shape[0]
+    pairs = blocks * (blocks + 1) // 2
+    number = src_block[...]
+    front_of = sum((number >= pairs * f).astype(jnp.int32) for f in range(1, fronts))
+    within = number - pairs * front_of
+    upper = sum((within >= a * (a + 1) // 2).astype(jnp.int32) for a in range(1, blocks))
+    lower = within - sum((upper >= a).astype(jnp.int32) * a for a in range(1, blocks))
+    code = (front_of * blocks + upper) * blocks + lower
+    live = lax.broadcasted_iota(jnp.int32, (1, slots), 1) < counts[0]
+    mark = jnp.where(live, target[...] + 1, 0)
+    named = lax.broadcasted_iota(jnp.int32, (ranks, slots), 0) == owner_of[...]
+
+    def per_owner(value):
+        found = jnp.sum(jnp.where(named, value, 0), axis=1, keepdims=True)
+        return jnp.broadcast_to(found, (ranks, 128))
+
+    label[...] = per_owner(mark)
+    row[...] = per_owner(code).T[0:1, :]
+    table = pltpu.make_async_copy(row, chosen, row_sem)
+    table.start()
 
     def remote(src, dst, send, recv, where):
         return pltpu.make_async_remote_copy(
@@ -65,72 +95,68 @@
             device_id=where, device_id_type=MESH,
         )
 
+    def wait(ref, sem):
+        pltpu.make_async_copy(ref, ref, sem).wait()
+
     def dn_row(i):
         return (i + chunks // 2) % chunks * UNIT
 
     y_copy = []
     for i in range(chunks):
-        up_at, dn_at = pl.ds(dn_row(i), UNIT), pl.ds(i * UNIT, UNIT)
         y_copy.append([
             remote(
-                own.at[:, :, up_at], from_dn.at[i], y_send.at[i, UP], y_recv.at[i, UP], to_y[UP]
+                own.at[:, :, pl.ds(dn_row(i), UNIT)], gathered.at[i, DOWN],
+                y_send, y_recv.at[i], to_y[UP],
             ),
             remote(
-                own.at[:, :, dn_at], from_up.at[i], y_send.at[i, DOWN], y_recv.at[i, DOWN],
-                to_y[DOWN],
+                own.at[:, :, pl.ds(i * UNIT, UNIT)], gathered.at[i, UP],
+                y_send, y_recv.at[i], to_y[DOWN],
             ),
         ])
     l_copy = [
-        remote(label, lab_in.at[i], l_send.at[i], l_recv.at[i], where)
+        remote(label, lab_in.at[i], l_send, l_recv, where)
         for i, where in enumerate([to_core] + to_pair[0] + to_pair[1])
     ]
-    for copy in l_copy:
-        copy.start()
-    load.wait()
-    for row in y_copy:
-        for copy in row:
-            copy.start()
-
     x_copy = [
         [
-            [
-                remote(
-                    xs.at[u, v, d], xr.at[u, v, d + 1], x_send.at[u, v, d], x_recv.at[u, v, d],
-                    ([to_core] + to_pair[v])[d],
-                )
-                for d in range(3)
-            ]
+            remote(
+                xs.at[u, v, d], xr.at[u, v, d + 1], x_send, x_recv.at[u],
+                ([to_core] + to_pair[v])[d],
+            )
+            for v in range(2)
+            for d in (1, 2, 0)
+        ]
+        for u in range(units)
+    ]
+    rank = [kinds[:u].count(kinds[u]) for u in range(units)]
+    kind = ["AE".index(letter) for letter in kinds]
+    sent, come = [ps, fs], [pr, fr]
+    p_copy = [
+        [
+            remote(
+                sent[kind[u]].at[rank[u], v], come[kind[u]].at[rank[u], v],
+                p_send.at[kind[u]], p_recv.at[u], to_pair[1 - v][0],
+            )
             for v in range(2)
         ]
         for u in range(units)
     ]
-    rank = [kinds[:u].count(kinds[u]) for u in range(units)]
-    p_copy = []
-    for u in range(units):
-        src, dst = (ps, pr) if kinds[u] == "A" else (fs, fr)
-        p_copy.append([
-            remote(
-                src.at[rank[u], v], dst.at[rank[u], v], p_send.at[u, v], p_recv.at[u, v],
-                to_pair[1 - v][0],
-            )
-            for v in range(2)
-        ])
-    z_copy = []
-    for u in range(units):
-        row = []
-        for way in range(2):
-            hops = []
-            for d in range(1, 5):
-                at = (way, d - 1) if d < 4 else (way, d - 1, way)
-                hops.append(remote(
-                    zs[u].at[at], zr[u].at[at], z_send.at[u, way, d - 1],
-                    z_recv.at[u, way, d - 1], to_z[way],
-                ))
-            row.append(hops)
-        z_copy.append(row)
+
+    def z_copy(u, way, d):
+        n, r = kind[u], rank[u]
+        if d == 4:
+            src, dst, sem = z4s[n].at[r, way], z4r[n].at[r, way], z_send.at[n, 1]
+        else:
+            src, dst, sem = z3s[n].at[r, way, d - 1], z3r[n].at[r, way, d - 1], z_send.at[n, 0]
+        return remote(src, dst, sem, z_recv.at[u, d - 1], to_z[way])
+
+    def wait_z(u, d):
+        n, r = kind[u], rank[u]
+        wait(z4r[n].at[r] if d == 4 else z3r[n].at[r, :, d - 1], z_recv.at[u, d - 1])
+
     k_copy = [
         [
-            remote(ks.at[i], kr.at[way, i], k_send.at[i, way], k_recv.at[i, way], to_y[way])
+            remote(ks.at[i], kr.at[way, i], k_send, k_recv, to_y[way])
             for way in range(2)
         ]
         for i in range(chunks)
@@ -154,22 +180,21 @@
             for i in range(max(chunk, chunks // 2 - 1 if meeting else 0) + 1):
                 if i not in arrived:
                     arrived.add(i)
-                    for copy in y_copy[i]:
-                        copy.wait_recv()
+                    wait(gathered.at[i], y_recv.at[i])
 
         def front(f, carry):
             def rows_of(b):
                 if own_rows:
                     return [own[f, b, group * 2 * UNIT:(group + 1) * 2 * UNIT, :]]
                 if meeting:
-                    return [from_dn[chunk, f, b], from_up[chunk, f, b]]
-                return [from_up[chunk, f, b], from_dn[chunk, f, b]]
+                    return [gathered[chunk, DOWN, f, b], gathered[chunk, UP, f, b]]
+                return [gathered[chunk, UP, f, b], gathered[chunk, DOWN, f, b]]
 
             def lanes_of(a):
                 if not meeting:
                     return [own[f, a]]
                 half = range(chunks // 2)
-                return [from_up[i, f, a] for i in half] + [from_dn[i, f, a] for i in half]
+                return [gathered[i, way, f, a] for way in (UP, DOWN) for i in half]
 
             for half in range(blocks // 2):
                 top = 2 * (half + 1)
@@ -199,11 +224,11 @@
             return carry
 
         lax.fori_loop(0, fronts, front, 0)
-        if meeting:
-            pack(3 * chunks + chunk, 0)
-        else:
-            pack(2 * group, 0)
-            pack(2 * group + 1, UNIT)
+
+    def members_of(group):
+        if group < 2 + chunks:
+            return [2 * group, 2 * group + 1]
+        return [3 * chunks + group - 2 - chunks]
 
     def pack(u, first):
         def slot(j, carry):
@@ -219,13 +244,9 @@
             return carry
 
         lax.fori_loop(0, 2 * RING_Z, slot, 0)
-        for v in range(2):
-            for d in (1, 2, 0):
-                x_copy[u][v][d].start()
 
     def weigh():
-        for copy in l_copy:
-            copy.wait_recv()
+        wait(lab_in, l_recv)
 
         def slot(j, carry):
             column, r = j // RING_Z, j % RING_Z
@@ -269,9 +290,10 @@
     columns = {"A": 1, "E": 2}
 
     def wait_x(u):
-        for v in range(2):
-            for copy in x_copy[u][v]:
-                copy.wait_recv()
+        wait(xs.at[u], x_recv.at[u])
+
+    def wait_p(u):
+        wait(come[kind[u]].at[rank[u]], p_recv.at[u])
 
     def pass_on(u):
         wait_x(u)
@@ -291,22 +313,26 @@
         wide = columns[kinds[u]]
         if step == 0:
             if kinds[u] == "A":
-                for copy in p_copy[u]:
-                    copy.wait_recv()
+                wait_p(u)
             else:
                 wait_x(u)
+        else:
+            wait_z(u, d + 1)
         for way in range(2):
             r = d if way == UP else RING_Z - d
-            if step > 0:
-                z_copy[u][way][d].wait_recv()
 
             def add(v, column, more):
                 total = both(u, v, column, r)
                 for t in range(targets):
                     value = total[t]
-                    if more:
-                        value = value + widen(zr[u][way, d, v, column, t])
-                    zs[u][way, d - 1, v, column, t] = narrow(value)
+                    if more and d == 3:
+                        value = value + widen(z4r[kind[u]][rank[u], way, column, t])
+                    elif more:
+                        value = value + widen(z3r[kind[u]][rank[u], way, d, v, column, t])
+                    if d == 4:
+                        z4s[kind[u]][rank[u], way, column, t] = narrow(value)
+                    else:
+                        z3s[kind[u]][rank[u], way, d - 1, v, column, t] = narrow(value)
 
             if d >= 3:
                 for v in range(2):
@@ -324,7 +350,7 @@
                     return carry
 
                 lax.fori_loop(0, 2 * wide, body, 0)
-            z_copy[u][way][d - 1].start()
+            z_copy(u, way, d).start()
 
     def settle(u, v, total):
         for t in range(targets):
@@ -351,14 +377,13 @@
                 write(piece)
 
     def end(u):
-        for way in range(2):
-            z_copy[u][way][0].wait_recv()
+        wait_z(u, 1)
         for column in reversed(range(columns[kinds[u]])):
             for v in range(2):
                 total = both(u, v, column, 0)
                 total = [
-                    total[t] + widen(zr[u][UP, 0, v, column, t])
-                    + widen(zr[u][DOWN, 0, v, column, t])
+                    total[t] + widen(z3r[kind[u]][rank[u], UP, 0, v, column, t])
+                    + widen(z3r[kind[u]][rank[u], DOWN, 0, v, column, t])
                     for t in range(targets)
                 ]
                 if column == 1:
@@ -379,8 +404,8 @@
         return row_of(u) if u < 3 * chunks else 3 * quarter + (u - 3 * chunks) * UNIT
 
     def join(u):
+        wait_p(u)
         for v in range(2):
-            p_copy[u][v].wait_recv()
             row = row_held(u) + v * HALF
             settle(u, v, [
                 summed[t, row:row + HALF].reshape(tile) + widen(fr[rank[u], v, t])
@@ -405,11 +430,28 @@
                 total = summed[t, piece * quarter:(piece + 1) * quarter]
             out[t, :, at] = total.T
 
+    def ship(group):
+        for i, u in enumerate(members_of(group)):
+            pack(u, i * UNIT)
+            for copy in x_copy[u]:
+                copy.start()
+
+    load.wait()
+    make(ORDER[0] // 8)
+    table.wait()
+    pl.semaphore_wait(barrier, len(peers))
+    for copies in y_copy:
+        for copy in copies:
+            copy.start()
+    for copy in l_copy:
+        copy.start()
+    ship(ORDER[0] // 8)
     weighed = False
-    for item in ORDER:
+    for item in ORDER[1:]:
         u, what = item // 8, item % 8
         if what == MAKE:
             make(u)
+            ship(u)
             continue
         if not weighed:
             weigh()
@@ -422,80 +464,71 @@
             end(u)
         else:
             hop(u, what)
-    for row in k_copy:
-        for copy in row:
-            copy.wait_recv()
+    wait(kr, k_recv)
     write(3)
-    for row in y_copy + p_copy + k_copy:
-        for copy in row:
-            copy.wait_send()
-    for copy in l_copy:
-        copy.wait_send()
-    for u in range(units):
-        for row in x_copy[u] + z_copy[u]:
-            for copy in row:
-                copy.wait_send()
-
-
-def assemble(chosen, label, panels, targets):
+    wait(gathered, y_send)
+    wait(lab_in, l_send)
+    wait(xs, x_send)
+    wait(kr, k_send)
+    for n in range(2):
+        if n in kind:
+            wait(sent[n], p_send.at[n])
+            wait(z3s[n], z_send.at[n, 0])
+            wait(z4s[n], z_send.at[n, 1])
+
+
+def assemble(counts, src_block, owner_of, target, panels, targets):
     fronts, blocks, quarter, width = panels.shape
     kinds = KINDS
     units = len(kinds)
     chunks = quarter // UNIT
+    ranks = 2 * RING_X * RING_Z
     bf16, f32 = jnp.bfloat16, jnp.float32
     dma = pltpu.SemaphoreType.DMA
     vmem = pltpu.VMEM
-    hops = [
-        vmem((2, 4, 2, 1 if kind == "A" else 2, targets, HALF, quarter), bf16) for kind in kinds
-    ]
-    passed = vmem((max(1, kinds.count("A")), 2, RING_Z, targets, HALF, quarter), bf16)
-    joined = vmem((max(1, kinds.count("E")), 2, targets, HALF, quarter), bf16)
-    gathered = vmem((chunks, fronts, blocks, UNIT, width), bf16)
+    block = (targets, HALF, quarter)
+    number = [max(1, kinds.count(letter)) for letter in "AE"]
+    three = [vmem((number[n], 2, 3, 2, n + 1) + block, bf16) for n in range(2)]
+    four = [vmem((number[n], 2, n + 1) + block, bf16) for n in range(2)]
+    passed = vmem((number[0], 2, RING_Z) + block, bf16)
+    joined = vmem((number[1], 2) + block, bf16)
     arrays = pl.BlockSpec(memory_space=vmem)
     return pl.pallas_call(
         functools.partial(kernel, kinds),
         out_shape=jax.ShapeDtypeStruct((targets, quarter, 4 * quarter), f32),
-        in_specs=[
-            pl.BlockSpec(memory_space=pltpu.SMEM), arrays, pl.BlockSpec(memory_space=pl.ANY)
-        ],
+        in_specs=[pl.BlockSpec(memory_space=pltpu.HBM)] * 5,
         out_specs=arrays,
         scratch_shapes=[
-            vmem(panels.shape, bf16), gathered, gathered,
-            vmem((5,) + label.shape, jnp.int32),
+            pltpu.SMEM(counts.shape, jnp.int32),
+            vmem(src_block.shape, jnp.int32), vmem(src_block.shape, jnp.int32),
+            vmem(src_block.shape, jnp.int32),
+            vmem(panels.shape, bf16),
+            vmem((chunks, 2, fronts, blocks, UNIT, width), bf16),
+            vmem((ranks, 128), jnp.int32),
+            vmem((5, ranks, 128), jnp.int32),
+            vmem((1, ranks), jnp.int32),
+            pltpu.SMEM((1, ranks), jnp.int32),
             vmem((2, 4, 2 * RING_Z, targets, 8, 128), f32),
             vmem((fronts * blocks * blocks, 2 * UNIT, quarter), bf16),
             vmem((units, 2, 3, 2 * RING_Z, HALF, quarter), bf16),
             vmem((units, 2, 4, 2 * RING_Z, HALF, quarter), bf16),
-            passed, passed, joined, joined, hops, hops,
+            passed, passed, joined, joined, three, three, four, four,
             vmem((chunks, targets, UNIT, quarter), bf16),
             vmem((2, chunks, targets, UNIT, quarter), bf16),
             vmem((targets, 4 * quarter, quarter), f32),
-            dma, dma((chunks, 2)), dma((chunks, 2)), dma((5,)), dma((5,)),
-            dma((units, 2, 3)), dma((units, 2, 3)), dma((units, 2)), dma((units, 2)),
-            dma((units, 2, 4)), dma((units, 2, 4)), dma((chunks, 2)), dma((chunks, 2)),
+            dma((4,)), dma, dma, dma, dma((chunks,)), dma, dma, dma, dma((units,)), dma((2,)),
+            dma((units,)), dma((2, 2)), dma((units, 4)), dma, dma,
         ],
         compiler_params=pltpu.CompilerParams(
-            collective_id=0, has_side_effects=True, vmem_limit_bytes=63 * 1024 * 1024
+            collective_id=0, has_side_effects=True, vmem_limit_bytes=62 * 1024 * 1024
         ),
-    )(chosen, label, panels)
+    )(counts, src_block, owner_of, target, panels)
 
 
 def per_device(panels, parent, src_block, dest_owner, target, counts):
-    blocks = panels.shape[1]
-    pairs = blocks * (blocks + 1) // 2
-    peers = lax.axis_size("col")
     slots = src_block.shape[1]
-    named = dest_owner.reshape(1, slots) == jnp.arange(peers, dtype=jnp.int32)[:, None]
-    within = src_block % pairs
-    upper = sum((within >= a * (a + 1) // 2).astype(jnp.int32) for a in range(1, blocks))
-    lower = within - upper * (upper + 1) // 2
-    code = (src_block // pairs * blocks + upper) * blocks + lower
-    chosen = jnp.sum(jnp.where(named, code, 0), axis=1)
-    live = jnp.arange(slots, dtype=jnp.int32) < counts[0]
-    mark = jnp.where(live, target + 1, 0).reshape(1, slots)
-    label = jnp.sum(jnp.where(named, mark, 0), axis=1)
     total = assemble(
-        chosen.reshape(1, peers), jnp.broadcast_to(label[:, None], (peers, 128)), panels,
+        counts, src_block, dest_owner.reshape(1, slots), target.reshape(1, slots), panels,
         parent.shape[0],
     )
     return parent - total

time: 109 us -> 103 us (0.945)
  other arithmetic: 5.4 us -> 2.4 us
  Pallas kernels: 102 us -> 99.4 us
    pallas_call x1, Pallas kernels: 102 us -> 99.4 us  [assemble(): pl.pallas_call(functools.partial(kernel, kinds), out_shape=jax.ShapeDtype...]
    reduce_sum x1 -> x0, other arithmetic: 1.34 us -> none  [per_device(): label = jnp.sum(jnp.where(named, mark, 0), axis=1)]
where the time goes in v3:
time: 103 us
  Pallas kernels  99.4 us (97%)
  other arithmetic  2.4 us (2%)
    pallas_call x1, Pallas kernels, assemble(): pl.pallas_call(functools.partial(kernel, kinds), out_shape=jax.ShapeDtype...  99.4 us
    sub x1, other arithmetic, per_device(): return parent - total  2.4 us

profile of v3, /device:TPU:8, one launch (start us, length us, event | category | flops | bytes accessed | tf_op | source)
XLA Modules:
  0.0 102.5 jit_solution(2075121201100462943)
XLA Ops:
  0.0 0.0 copy-start
  0.7 99.4 %shard_map.64 = f32[4,128,512]{2,1,0:T(8,128)} custom-call(s32[1]{0:T(128)S(6)} %copy.7.counts_in, s32[1,40]{1,0:T(1,128)} %src_block_in.1, s32[1,40]{1,0:T(1,128)} %bitcast.2, s32[1,40]{1,0:T(1,128)} %bitcast.3, bf16[4,4,128,512]{3,2,1,0:T(8,128)(2,1)} %panels.1), custom_call_target="tpu_custom_call" | custom-call | tf_op jit(solution)/shard_map/pallas_call | solution.py:496
  100.1 0.0 copy-done
  100.1 2.4 %sub.3 = f32[4,128,512]{2,1,0:T(8,128)} subtract(f32[4,128,512]{2,1,0:T(8,128)S(1)} %copy-done, f32[4,128,512]{2,1,0:T(8,128)} %shard_map.64) | non-fusion elementwise | flops 262144 | bytes 3145728 | tf_op jit(solution)/shard_map/sub | solution.py:534
Async XLA Ops:
  0.0 100.1 %copy-start = (f32[4,128,512]{2,1,0:T(8,128)S(1)}, f32[4,128,512]{2,1,0:T(8,128)}, u32[]{:S(2)}) copy-start(f32[4,128,512]{2,1,0:T(8,128)} %param.7) | copy-start | bytes 3145732

commit v4 on v3

--- a/solution.py
+++ b/solution.py
@@ -9,16 +9,16 @@
 
 MESH = pl.DeviceIdType.MESH
 
-KINDS = "EEEAEAEEEEAAEEAA"
+KINDS = "EEEEAAEEEEAAAEAE"
 MAKE, PASS, JOIN = 5, 6, 7
 ORDER = [
-    5, 13, 0, 1, 8, 16, 2, 21, 9, 30, 17, 3, 10, 32, 18, 4,
-    46, 11, 33, 29, 24, 19, 61, 40, 25, 34, 12, 53, 48, 41, 26, 7,
-    20, 35, 56, 49, 42, 27, 69, 15, 57, 104, 36, 37, 96, 50, 43, 23,
-    28, 58, 105, 118, 97, 39, 51, 44, 64, 59, 77, 106, 72, 45, 98, 52,
-    65, 112, 60, 107, 126, 73, 99, 86, 66, 113, 108, 94, 55, 63, 74, 100,
-    120, 67, 114, 75, 121, 80, 111, 68, 115, 88, 76, 103, 71, 122, 81, 116,
-    89, 79, 123, 82, 90, 124, 83, 91, 84, 92,
+    5, 29, 21, 13, 0, 37, 24, 1, 16, 25, 45, 8, 17, 2, 26, 38,
+    9, 53, 18, 46, 3, 27, 32, 10, 61, 48, 19, 109, 28, 33, 4, 40,
+    101, 49, 56, 69, 34, 20, 41, 11, 104, 31, 7, 50, 57, 77, 42, 102,
+    35, 117, 105, 12, 64, 51, 23, 85, 58, 43, 72, 36, 106, 65, 96, 52,
+    93, 125, 15, 73, 59, 118, 44, 107, 86, 66, 97, 55, 74, 94, 60, 108,
+    120, 67, 98, 75, 112, 121, 68, 99, 80, 76, 113, 88, 122, 63, 111, 100,
+    71, 81, 79, 114, 89, 123, 82, 115, 90, 124, 83, 116, 91, 127, 84, 92,
 ]
 HALF = 16
 UNIT = 2 * HALF
@@ -27,8 +27,8 @@
 
 
 def kernel(
-    kinds, counts_in, src_block_in, owner_in, target_in, panels, out,
-    counts, src_block, owner_of, target, own, gathered, label, lab_in, row, chosen, weight, product, xs, xr, ps, pr, fs, fr,
+    kinds, counts_in, listed_in, panels, out,
+    counts, listed, own, gathered, label, lab_in, row, chosen, weight, product, xs, xr, ps, pr, fs, fr,
     z3s, z3r, z4s, z4r, ks, kr, summed,
     list_sem, own_sem, row_sem, y_send, y_recv, l_send, l_recv, x_send, x_recv, p_send, p_recv,
     z_send, z_recv, k_send, k_recv,
@@ -36,18 +36,15 @@
     fronts, blocks, quarter, width = own.shape
     targets = out.shape[0]
     units = len(kinds)
-    chunks = quarter // UNIT
+    chunks, meets = quarter // HALF, quarter // UNIT
     g, c = lax.axis_index("grp"), lax.axis_index("col")
     x, z, k = c // (2 * RING_Z), (c // 2) % RING_Z, c % 2
     pair = [x + 1 - 2 * (x % 2), 3 - x]
     across = (x + 2) % RING_X
 
     lists = [
-        pltpu.make_async_copy(src, dst, list_sem.at[i])
-        for i, (src, dst) in enumerate([
-            (counts_in, counts), (src_block_in, src_block), (owner_in, owner_of),
-            (target_in, target),
-        ])
+        pltpu.make_async_copy(counts_in, counts, list_sem.at[0]),
+        pltpu.make_async_copy(listed_in, listed, list_sem.at[1]),
     ]
     load = pltpu.make_async_copy(panels, own, own_sem)
     for copy in lists + [load]:
@@ -68,17 +65,17 @@
 
     for copy in lists:
         copy.wait()
-    slots, ranks = src_block.shape[1], label.shape[0]
+    slots, ranks = listed.shape[1], label.shape[0]
     pairs = blocks * (blocks + 1) // 2
-    number = src_block[...]
+    number = listed[0:1]
     front_of = sum((number >= pairs * f).astype(jnp.int32) for f in range(1, fronts))
     within = number - pairs * front_of
     upper = sum((within >= a * (a + 1) // 2).astype(jnp.int32) for a in range(1, blocks))
     lower = within - sum((upper >= a).astype(jnp.int32) * a for a in range(1, blocks))
     code = (front_of * blocks + upper) * blocks + lower
     live = lax.broadcasted_iota(jnp.int32, (1, slots), 1) < counts[0]
-    mark = jnp.where(live, target[...] + 1, 0)
-    named = lax.broadcasted_iota(jnp.int32, (ranks, slots), 0) == owner_of[...]
+    mark = jnp.where(live, listed[2:3] + 1, 0)
+    named = lax.broadcasted_iota(jnp.int32, (ranks, slots), 0) == listed[1:2]
 
     def per_owner(value):
         found = jnp.sum(jnp.where(named, value, 0), axis=1, keepdims=True)
@@ -99,17 +96,17 @@
         pltpu.make_async_copy(ref, ref, sem).wait()
 
     def dn_row(i):
-        return (i + chunks // 2) % chunks * UNIT
+        return (i + chunks // 2) % chunks * HALF
 
     y_copy = []
     for i in range(chunks):
         y_copy.append([
             remote(
-                own.at[:, :, pl.ds(dn_row(i), UNIT)], gathered.at[i, DOWN],
+                own.at[:, :, pl.ds(dn_row(i), HALF)], gathered.at[i, DOWN],
                 y_send, y_recv.at[i], to_y[UP],
             ),
             remote(
-                own.at[:, :, pl.ds(i * UNIT, UNIT)], gathered.at[i, UP],
+                own.at[:, :, pl.ds(i * HALF, HALF)], gathered.at[i, UP],
                 y_send, y_recv.at[i], to_y[DOWN],
             ),
         ])
@@ -159,42 +156,45 @@
             remote(ks.at[i], kr.at[way, i], k_send, k_recv, to_y[way])
             for way in range(2)
         ]
-        for i in range(chunks)
+        for i in range(meets)
     ]
 
-    def row_of(u):
-        if u < chunks:
-            return u * UNIT
-        chunk, side = (u - chunks) // 2, (u - chunks) % 2
-        return quarter + chunk * UNIT if side == 0 else 2 * quarter + dn_row(chunk)
+    def row_of(u, v):
+        if meets <= u < meets + chunks:
+            return quarter + (u - meets) * HALF if v == 0 else 2 * quarter + dn_row(u - meets)
+        return (u if u < meets else u - chunks + 2 * meets) * UNIT + v * HALF
 
     def owner(column, r):
         return column * (2 * RING_Z) + ((z + r) % RING_Z) * 2
 
     arrived = set()
 
-    def make(group):
-        chunk = group - 2 if group < 2 + chunks else group - 2 - chunks
-        own_rows, meeting = group < 2, group >= 2 + chunks
-        if not own_rows:
-            for i in range(max(chunk, chunks // 2 - 1 if meeting else 0) + 1):
-                if i not in arrived:
-                    arrived.add(i)
-                    wait(gathered.at[i], y_recv.at[i])
+    def make(u):
+        meeting, chunk = u >= meets + chunks, u - meets
+        if meeting:
+            first = 2 * (u - meets - chunks)
+            last = max(first + 1, chunks // 2 - 1)
+        else:
+            last = chunk
+        for i in range(last + 1):
+            if i not in arrived:
+                arrived.add(i)
+                wait(gathered.at[i], y_recv.at[i])
+        stride = 2 * UNIT if meeting else UNIT
 
         def front(f, carry):
             def rows_of(b):
-                if own_rows:
-                    return [own[f, b, group * 2 * UNIT:(group + 1) * 2 * UNIT, :]]
                 if meeting:
-                    return [gathered[chunk, DOWN, f, b], gathered[chunk, UP, f, b]]
+                    two = (first, first + 1)
+                    return [gathered[i, way, f, b] for way in (DOWN, UP) for i in two]
+                if u < meets:
+                    return [own[f, b, u * UNIT:(u + 1) * UNIT, :]]
                 return [gathered[chunk, UP, f, b], gathered[chunk, DOWN, f, b]]
 
             def lanes_of(a):
                 if not meeting:
                     return [own[f, a]]
-                half = range(chunks // 2)
-                return [gathered[i, way, f, a] for way in (UP, DOWN) for i in half]
+                return [gathered[i, way, f, a] for way in (UP, DOWN) for i in range(chunks // 2)]
 
             for half in range(blocks // 2):
                 top = 2 * (half + 1)
@@ -207,36 +207,27 @@
                 )
                 for i in range(2):
                     a = 2 * half + i
+                    lanes = slice(i * quarter, (i + 1) * quarter)
                     for b in range(a + 1):
-                        at = 2 * b * UNIT
-                        lanes = slice(i * quarter, (i + 1) * quarter)
+                        value = made[b * stride:b * stride + UNIT, lanes]
                         if meeting:
-                            first = lax.broadcasted_iota(
+                            near_half = lax.broadcasted_iota(
                                 jnp.int32, (UNIT, quarter), 1
                             ) < quarter // 2
-                            product[(f * blocks + a) * blocks + b, :UNIT] = jnp.where(
-                                first, made[at:at + UNIT, lanes], made[at + UNIT:at + 2 * UNIT, lanes]
-                            ).astype(jnp.bfloat16)
-                        else:
-                            product[(f * blocks + a) * blocks + b] = made[
-                                at:at + 2 * UNIT, lanes
-                            ].astype(jnp.bfloat16)
+                            other = made[b * stride + UNIT:(b + 1) * stride, lanes]
+                            value = jnp.where(near_half, value, other)
+                        product[(f * blocks + a) * blocks + b] = value.astype(jnp.bfloat16)
             return carry
 
         lax.fori_loop(0, fronts, front, 0)
 
-    def members_of(group):
-        if group < 2 + chunks:
-            return [2 * group, 2 * group + 1]
-        return [3 * chunks + group - 2 - chunks]
-
-    def pack(u, first):
+    def pack(u):
         def slot(j, carry):
             column, r = j // RING_Z, j % RING_Z
             for v in range(2):
                 here = owner(x + column * (pair[1 - v] - x), r)
                 there = owner(pair[v] + column * (across - pair[v]), r)
-                rows = slice(first + v * HALF, first + (v + 1) * HALF)
+                rows = slice(v * HALF, (v + 1) * HALF)
                 xr[u, v, 0, j] = product[chosen[0, here + k], rows, :]
                 xs[u, v, 0, j] = product[chosen[0, here + 1 - k], rows, :]
                 xs[u, v, 1, j] = product[chosen[0, there + k], rows, :]
@@ -355,26 +346,25 @@
     def settle(u, v, total):
         for t in range(targets):
             value = total[t].reshape(HALF, 128)
-            if u >= 3 * chunks:
-                ks[u - 3 * chunks, t, v * HALF:(v + 1) * HALF] = value.astype(jnp.bfloat16)
+            if u >= meets + chunks:
+                ks[u - meets - chunks, t, v * HALF:(v + 1) * HALF] = value.astype(jnp.bfloat16)
             else:
-                row = row_of(u) + v * HALF
+                row = row_of(u, v)
                 summed[t, row:row + HALF] = value
 
-    done = []
+    done = set()
 
     def finished(u):
-        done.append(u)
-        if u >= 3 * chunks:
-            for copy in k_copy[u - 3 * chunks]:
+        done.add(u)
+        if u >= meets + chunks:
+            for copy in k_copy[u - meets - chunks]:
                 copy.start()
-        for piece in range(3):
-            if piece == 0:
-                members = list(range(chunks))
-            else:
-                members = list(range(chunks + piece - 1, 3 * chunks, 2))
-            if u in members and all(i in done for i in members):
-                write(piece)
+        elif u < meets:
+            if all(i in done for i in range(meets)):
+                write(0)
+        elif all(i in done for i in range(meets, meets + chunks)):
+            write(1)
+            write(2)
 
     def end(u):
         wait_z(u, 1)
@@ -393,20 +383,16 @@
                 elif kinds[u] == "A":
                     settle(u, v, total)
                 else:
+                    row = row_of(u, v)
                     for t in range(targets):
-                        summed[t, row_held(u) + v * HALF:row_held(u) + (v + 1) * HALF] = total[
-                            t
-                        ].reshape(HALF, 128)
+                        summed[t, row:row + HALF] = total[t].reshape(HALF, 128)
         if kinds[u] == "A":
             finished(u)
-
-    def row_held(u):
-        return row_of(u) if u < 3 * chunks else 3 * quarter + (u - 3 * chunks) * UNIT
 
     def join(u):
         wait_p(u)
         for v in range(2):
-            row = row_held(u) + v * HALF
+            row = row_of(u, v)
             settle(u, v, [
                 summed[t, row:row + HALF].reshape(tile) + widen(fr[rank[u], v, t])
                 for t in range(targets)
@@ -419,10 +405,10 @@
         at = pl.ds(pl.multiple_of(member[piece] * quarter, quarter), quarter)
         for t in range(targets):
             if piece == 3:
-                order = [(i + chunks // 2) % chunks for i in range(chunks)]
+                order = [(i + meets // 2) % meets for i in range(meets)]
                 below = jnp.concatenate([kr[UP, i, t].astype(jnp.float32) for i in order], axis=0)
                 above = jnp.concatenate(
-                    [kr[DOWN, i, t].astype(jnp.float32) for i in range(chunks)], axis=0
+                    [kr[DOWN, i, t].astype(jnp.float32) for i in range(meets)], axis=0
                 )
                 first = lax.broadcasted_iota(jnp.int32, (quarter, quarter), 1) < quarter // 2
                 total = jnp.where(first, below, above)
@@ -430,11 +416,10 @@
                 total = summed[t, piece * quarter:(piece + 1) * quarter]
             out[t, :, at] = total.T
 
-    def ship(group):
-        for i, u in enumerate(members_of(group)):
-            pack(u, i * UNIT)
-            for copy in x_copy[u]:
-                copy.start()
+    def ship(u):
+        pack(u)
+        for copy in x_copy[u]:
+            copy.start()
 
     load.wait()
     make(ORDER[0] // 8)
@@ -477,11 +462,11 @@
             wait(z4s[n], z_send.at[n, 1])
 
 
-def assemble(counts, src_block, owner_of, target, panels, targets):
+def assemble(counts, listed, panels, targets):
     fronts, blocks, quarter, width = panels.shape
     kinds = KINDS
     units = len(kinds)
-    chunks = quarter // UNIT
+    chunks, meets = quarter // HALF, quarter // UNIT
     ranks = 2 * RING_X * RING_Z
     bf16, f32 = jnp.bfloat16, jnp.float32
     dma = pltpu.SemaphoreType.DMA
@@ -496,41 +481,37 @@
     return pl.pallas_call(
         functools.partial(kernel, kinds),
         out_shape=jax.ShapeDtypeStruct((targets, quarter, 4 * quarter), f32),
-        in_specs=[pl.BlockSpec(memory_space=pltpu.HBM)] * 5,
+        in_specs=[pl.BlockSpec(memory_space=pltpu.HBM)] * 3,
         out_specs=arrays,
         scratch_shapes=[
-            pltpu.SMEM(counts.shape, jnp.int32),
-            vmem(src_block.shape, jnp.int32), vmem(src_block.shape, jnp.int32),
-            vmem(src_block.shape, jnp.int32),
+            pltpu.SMEM(counts.shape, jnp.int32), vmem(listed.shape, jnp.int32),
             vmem(panels.shape, bf16),
-            vmem((chunks, 2, fronts, blocks, UNIT, width), bf16),
+            vmem((chunks, 2, fronts, blocks, HALF, width), bf16),
             vmem((ranks, 128), jnp.int32),
             vmem((5, ranks, 128), jnp.int32),
             vmem((1, ranks), jnp.int32),
             pltpu.SMEM((1, ranks), jnp.int32),
             vmem((2, 4, 2 * RING_Z, targets, 8, 128), f32),
-            vmem((fronts * blocks * blocks, 2 * UNIT, quarter), bf16),
+            vmem((fronts * blocks * blocks, UNIT, quarter), bf16),
             vmem((units, 2, 3, 2 * RING_Z, HALF, quarter), bf16),
             vmem((units, 2, 4, 2 * RING_Z, HALF, quarter), bf16),
             passed, passed, joined, joined, three, three, four, four,
-            vmem((chunks, targets, UNIT, quarter), bf16),
-            vmem((2, chunks, targets, UNIT, quarter), bf16),
+            vmem((meets, targets, UNIT, quarter), bf16),
+            vmem((2, meets, targets, UNIT, quarter), bf16),
             vmem((targets, 4 * quarter, quarter), f32),
-            dma((4,)), dma, dma, dma, dma((chunks,)), dma, dma, dma, dma((units,)), dma((2,)),
+            dma((2,)), dma, dma, dma, dma((chunks,)), dma, dma, dma, dma((units,)), dma((2,)),
             dma((units,)), dma((2, 2)), dma((units, 4)), dma, dma,
         ],
         compiler_params=pltpu.CompilerParams(
-            collective_id=0, has_side_effects=True, vmem_limit_bytes=62 * 1024 * 1024
+            collective_id=0, has_side_effects=True, vmem_limit_bytes=52 * 1024 * 1024
         ),
-    )(counts, src_block, owner_of, target, panels)
+    )(counts, listed, panels)
 
 
 def per_device(panels, parent, src_block, dest_owner, target, counts):
     slots = src_block.shape[1]
-    total = assemble(
-        counts, src_block, dest_owner.reshape(1, slots), target.reshape(1, slots), panels,
-        parent.shape[0],
-    )
+    listed = jnp.concatenate([src_block, dest_owner.reshape(1, slots), target[None, :]])
+    total = assemble(counts, listed, panels, parent.shape[0])
     return parent - total
 
 

time: 103 us -> 96.8 us (0.940)
  Pallas kernels: 99.4 us -> 94 us
    pallas_call x1, Pallas kernels: 99.4 us -> 94 us  [assemble(): pl.pallas_call(functools.partial(kernel, kinds), out_shape=jax.ShapeDtype...]
    sub x1, other arithmetic: 2.4 us -> 1.18 us  [per_device(): return parent - total]
where the time goes in v4:
time: 96.8 us; the launch traced here: 96.7 us
  Pallas kernels  94 us (97%)
  other arithmetic  1.88 us (2%)
    pallas_call x1, Pallas kernels, assemble(): pl.pallas_call(functools.partial(kernel, kinds), out_shape=jax.ShapeDtype...  94 us

profile of v4, /device:TPU:8, one launch (start us, length us, event | category | flops | bytes accessed | tf_op | source)
XLA Modules:
  0.0 96.7 jit_solution(14049436925515377566)
XLA Ops:
  0.0 0.0 copy-start
  0.7 0.7 pad_add_fusion.listed_in
  1.4 94.0 %shard_map.64 = f32[4,128,512]{2,1,0:T(8,128)S(1)} custom-call(s32[1]{0:T(128)S(6)} %copy.7.counts_in, s32[3,40]{1,0:T(4,128)S(1)} %pad_add_fusion.listed_in, bf16[4,4,128,512]{3,2,1,0:T(8,128)(2,1)} %panels.1), custom_call_target="tpu_custom_call" | custom-call | tf_op jit(solution)/shard_map/pallas_call | solution.py:481
  95.5 0.0 copy-done
  95.5 1.2 %sub.3 = f32[4,128,512]{2,1,0:T(8,128)} subtract(f32[4,128,512]{2,1,0:T(8,128)S(1)} %copy-done, f32[4,128,512]{2,1,0:T(8,128)S(1)} %shard_map.64) | non-fusion elementwise | flops 262144 | bytes 3145728 | tf_op jit(solution)/shard_map/sub | solution.py:515
Async XLA Ops:
  0.0 95.5 %copy-start = (f32[4,128,512]{2,1,0:T(8,128)S(1)}, f32[4,128,512]{2,1,0:T(8,128)}, u32[]{:S(2)}) copy-start(f32[4,128,512]{2,1,0:T(8,128)} %param.7) | copy-start | bytes 3145732

commit v5 on v4

--- a/solution.py
+++ b/solution.py
@@ -12,13 +12,13 @@
 KINDS = "EEEEAAEEEEAAAEAE"
 MAKE, PASS, JOIN = 5, 6, 7
 ORDER = [
-    5, 29, 21, 13, 0, 37, 24, 1, 16, 25, 45, 8, 17, 2, 26, 38,
-    9, 53, 18, 46, 3, 27, 32, 10, 61, 48, 19, 109, 28, 33, 4, 40,
-    101, 49, 56, 69, 34, 20, 41, 11, 104, 31, 7, 50, 57, 77, 42, 102,
-    35, 117, 105, 12, 64, 51, 23, 85, 58, 43, 72, 36, 106, 65, 96, 52,
-    93, 125, 15, 73, 59, 118, 44, 107, 86, 66, 97, 55, 74, 94, 60, 108,
-    120, 67, 98, 75, 112, 121, 68, 99, 80, 76, 113, 88, 122, 63, 111, 100,
-    71, 81, 79, 114, 89, 123, 82, 115, 90, 124, 83, 116, 91, 127, 84, 92,
+    5, 21, 29, 0, 13, 16, 1, 37, 24, 17, 2, 8, 25, 45, 18, 38,
+    3, 9, 26, 46, 53, 19, 4, 10, 32, 27, 109, 101, 40, 48, 33, 11,
+    7, 61, 41, 104, 69, 49, 102, 12, 34, 28, 20, 42, 105, 56, 77, 50,
+    117, 64, 35, 106, 43, 57, 85, 51, 15, 96, 65, 31, 36, 23, 72, 107,
+    44, 125, 58, 118, 97, 93, 86, 73, 66, 52, 108, 120, 59, 98, 74, 67,
+    112, 121, 94, 60, 99, 75, 68, 113, 80, 55, 111, 122, 100, 76, 88, 63,
+    114, 71, 81, 123, 79, 89, 115, 82, 124, 90, 116, 83, 127, 91, 84, 92,
 ]
 HALF = 16
 UNIT = 2 * HALF
@@ -94,6 +94,15 @@
 
     def wait(ref, sem):
         pltpu.make_async_copy(ref, ref, sem).wait()
+
+    def parts(letter):
+        cut = RING_Z if letter == "A" else 6
+        return [pl.ds(0, cut), pl.ds(cut, 2 * RING_Z - cut)]
+
+    def slot_of(letter, column, r):
+        if letter == "A":
+            return (1 - column) * RING_Z + r
+        return 2 * [7, 5, 3, 1, 0, 2, 4, 6][r] + column
 
     def dn_row(i):
         return (i + chunks // 2) % chunks * HALF
@@ -117,11 +126,11 @@
     x_copy = [
         [
             remote(
-                xs.at[u, v, d], xr.at[u, v, d + 1], x_send, x_recv.at[u],
+                xs.at[u, v, d, part], xr.at[u, v, d + 1, part], x_send, x_recv.at[u, i],
                 ([to_core] + to_pair[v])[d],
             )
-            for v in range(2)
-            for d in (1, 2, 0)
+            for i, part in enumerate(parts(kinds[u]))
+            for v, d in ((0, 1), (0, 2), (1, 1), (1, 2), (0, 0), (1, 0))
         ]
         for u in range(units)
     ]
@@ -219,11 +228,16 @@
                         product[(f * blocks + a) * blocks + b] = value.astype(jnp.bfloat16)
             return carry
 
-        lax.fori_loop(0, fronts, front, 0)
+        lax.fori_loop(0, fronts, front, 0, unroll=True)
 
     def pack(u):
         def slot(j, carry):
-            column, r = j // RING_Z, j % RING_Z
+            if kinds[u] == "A":
+                column, r = 1 - j // RING_Z, j % RING_Z
+            else:
+                column, place = j % 2, j // 2
+                odd = place % 2
+                r = 4 + (1 - odd) * (place // 2) - odd * ((place + 1) // 2)
             for v in range(2):
                 here = owner(x + column * (pair[1 - v] - x), r)
                 there = owner(pair[v] + column * (across - pair[v]), r)
@@ -234,7 +248,7 @@
                 xs[u, v, 2, j] = product[chosen[0, there + 1 - k], rows, :]
             return carry
 
-        lax.fori_loop(0, 2 * RING_Z, slot, 0)
+        lax.fori_loop(0, 2 * RING_Z, slot, 0, unroll=2)
 
     def weigh():
         wait(lab_in, l_recv)
@@ -253,7 +267,7 @@
                         weight[v, s, j, t] = jnp.where(full == t + 1, 1.0, 0.0).astype(jnp.float32)
             return carry
 
-        lax.fori_loop(0, 2 * RING_Z, slot, 0)
+        lax.fori_loop(0, 2 * RING_Z, slot, 0, unroll=2)
 
     tile = (HALF // 8, 8, 128)
 
@@ -263,40 +277,41 @@
     def narrow(value):
         return value.reshape(HALF, 128).astype(jnp.bfloat16)
 
-    def near(u, v, j):
+    def near(u, v, column, r):
         total = [None] * targets
+        here, j = slot_of(kinds[u], column, r), column * RING_Z + r
         for s in range(4):
-            block = widen(xr[u, v, s, j])
+            block = widen(xr[u, v, s, here])
             for t in range(targets):
                 part = block * weight[v, s, j, t][None]
                 total[t] = part if s == 0 else total[t] + part
         return total
 
     def both(u, v, column, r):
-        total = near(u, v, column * RING_Z + r)
+        total = near(u, v, column, r)
         if kinds[u] == "A":
             total = [total[t] + widen(pr[rank[u], v, r, t]) for t in range(targets)]
         return total
 
     columns = {"A": 1, "E": 2}
 
-    def wait_x(u):
-        wait(xs.at[u], x_recv.at[u])
+    def wait_x(u, i):
+        wait(xs.at[u, :, :, parts(kinds[u])[i]], x_recv.at[u, i])
 
     def wait_p(u):
         wait(come[kind[u]].at[rank[u]], p_recv.at[u])
 
     def pass_on(u):
-        wait_x(u)
+        wait_x(u, 0)
 
         for v in range(2):
             def slot(r, carry):
-                total = near(u, v, RING_Z + r)
+                total = near(u, v, 1, r)
                 for t in range(targets):
                     ps[rank[u], v, r, t] = narrow(total[t])
                 return carry
 
-            lax.fori_loop(0, RING_Z, slot, 0)
+            lax.fori_loop(0, RING_Z, slot, 0, unroll=2)
             p_copy[u][v].start()
 
     def hop(u, step):
@@ -305,10 +320,13 @@
         if step == 0:
             if kinds[u] == "A":
                 wait_p(u)
+                wait_x(u, 1)
             else:
-                wait_x(u)
+                wait_x(u, 0)
         else:
             wait_z(u, d + 1)
+            if step == 2 and kinds[u] == "E":
+                wait_x(u, 1)
         for way in range(2):
             r = d if way == UP else RING_Z - d
 
@@ -334,13 +352,13 @@
                         add(v, column, d == 3 and v == way)
                         return carry
 
-                    lax.fori_loop(0, wide, body, 0)
+                    lax.fori_loop(0, wide, body, 0, unroll=True)
             else:
                 def body(j, carry):
                     add(j // wide, j % wide, True)
                     return carry
 
-                lax.fori_loop(0, 2 * wide, body, 0)
+                lax.fori_loop(0, 2 * wide, body, 0, unroll=True)
             z_copy(u, way, d).start()
 
     def settle(u, v, total):
@@ -499,7 +517,7 @@
             vmem((meets, targets, UNIT, quarter), bf16),
             vmem((2, meets, targets, UNIT, quarter), bf16),
             vmem((targets, 4 * quarter, quarter), f32),
-            dma((2,)), dma, dma, dma, dma((chunks,)), dma, dma, dma, dma((units,)), dma((2,)),
+            dma((2,)), dma, dma, dma, dma((chunks,)), dma, dma, dma, dma((units, 2)), dma((2,)),
             dma((units,)), dma((2, 2)), dma((units, 4)), dma, dma,
         ],
         compiler_params=pltpu.CompilerParams(

time: 96.8 us -> 94.7 us (0.978)
  Pallas kernels: 94 us -> 91.7 us
    pallas_call x1, Pallas kernels: 94 us -> 91.7 us  [assemble(): pl.pallas_call(functools.partial(kernel, kinds), out_shape=jax.ShapeDtype...]
where the time goes in v5:
time: 94.7 us; the launch traced here: 94.3 us
  Pallas kernels  91.7 us (97%)
  other arithmetic  1.88 us (2%)
    pallas_call x1, Pallas kernels, assemble(): pl.pallas_call(functools.partial(kernel, kinds), out_shape=jax.ShapeDtype...  91.7 us

profile of v5, /device:TPU:8, one launch (start us, length us, event | category | flops | bytes accessed | tf_op | source)
XLA Modules:
  0.0 94.3 jit_solution(10655243087963432560)
XLA Ops:
  0.0 0.0 copy-start
  0.7 0.7 pad_add_fusion.listed_in
  1.4 91.7 %shard_map.64 = f32[4,128,512]{2,1,0:T(8,128)S(1)} custom-call(s32[1]{0:T(128)S(6)} %copy.7.counts_in, s32[3,40]{1,0:T(4,128)S(1)} %pad_add_fusion.listed_in, bf16[4,4,128,512]{3,2,1,0:T(8,128)(2,1)} %panels.1), custom_call_target="tpu_custom_call" | custom-call | tf_op jit(solution)/shard_map/pallas_call | solution.py:499
  93.1 0.0 copy-done
  93.1 1.2 %sub.3 = f32[4,128,512]{2,1,0:T(8,128)} subtract(f32[4,128,512]{2,1,0:T(8,128)S(1)} %copy-done, f32[4,128,512]{2,1,0:T(8,128)S(1)} %shard_map.64) | non-fusion elementwise | flops 262144 | bytes 3145728 | tf_op jit(solution)/shard_map/sub | solution.py:533
Async XLA Ops:
  0.0 93.1 %copy-start = (f32[4,128,512]{2,1,0:T(8,128)S(1)}, f32[4,128,512]{2,1,0:T(8,128)}, u32[]{:S(2)}) copy-start(f32[4,128,512]{2,1,0:T(8,128)} %param.7) | copy-start | bytes 3145732

commit v6 on v5

--- a/solution.py
+++ b/solution.py
@@ -440,14 +440,14 @@
             copy.start()
 
     load.wait()
-    make(ORDER[0] // 8)
-    table.wait()
     pl.semaphore_wait(barrier, len(peers))
     for copies in y_copy:
         for copy in copies:
             copy.start()
     for copy in l_copy:
         copy.start()
+    make(ORDER[0] // 8)
+    table.wait()
     ship(ORDER[0] // 8)
     weighed = False
     for item in ORDER[1:]:

time: 94.7 us -> 94.7 us (level)
  no operation moved by 1% of the time
where the time goes in v6:
time: 94.7 us; the launch traced here: 94.2 us
  Pallas kernels  91.6 us (97%)
  other arithmetic  1.88 us (2%)
    pallas_call x1, Pallas kernels, assemble(): pl.pallas_call(functools.partial(kernel, kinds), out_shape=jax.ShapeDtype...  91.6 us

profile of v6, /device:TPU:8, one launch (start us, length us, event | category | flops | bytes accessed | tf_op | source)
XLA Modules:
  0.0 94.2 jit_solution(14425461898536131877)
XLA Ops:
  0.0 0.0 copy-start
  0.7 0.7 pad_add_fusion.listed_in
  1.4 91.6 %shard_map.64 = f32[4,128,512]{2,1,0:T(8,128)S(1)} custom-call(s32[1]{0:T(128)S(6)} %copy.7.counts_in, s32[3,40]{1,0:T(4,128)S(1)} %pad_add_fusion.listed_in, bf16[4,4,128,512]{3,2,1,0:T(8,128)(2,1)} %panels.1), custom_call_target="tpu_custom_call" | custom-call | tf_op jit(solution)/shard_map/pallas_call | solution.py:499
  93.0 0.0 copy-done
  93.0 1.2 %sub.3 = f32[4,128,512]{2,1,0:T(8,128)} subtract(f32[4,128,512]{2,1,0:T(8,128)S(1)} %copy-done, f32[4,128,512]{2,1,0:T(8,128)S(1)} %shard_map.64) | non-fusion elementwise | flops 262144 | bytes 3145728 | tf_op jit(solution)/shard_map/sub | solution.py:533
Async XLA Ops:
  0.0 93.0 %copy-start = (f32[4,128,512]{2,1,0:T(8,128)S(1)}, f32[4,128,512]{2,1,0:T(8,128)}, u32[]{:S(2)}) copy-start(f32[4,128,512]{2,1,0:T(8,128)} %param.7) | copy-start | bytes 3145732
